TPU v7x, 32 devices: a whole 2x2x4 slice. The times are simulated.
32 devices in a mesh: dp: 8 (over z, x), ctx: 2 (over core), tensor: 2 (over y).
Axes of the slice: x: 2, y: 2, z: 4, core: 2. Of those that a mesh axis runs over, the one named last changes fastest.
Arguments:
- tokens: bfloat16 [16, 736, 1152], P(('dp', 'tensor'), 'ctx'), may hold values from -6 to 6
- teacher: bfloat16 [16, 736, 1152], P(('dp', 'tensor'), 'ctx'), may hold values from -6 to 6
- valid_len: int32 [16], P(('dp', 'tensor')), may hold values from 0 to 729, as said below
- ln1_gain: bfloat16 [1152], P(('dp', 'ctx')), may hold values from 0.5 to 1.5
- ln1_bias: bfloat16 [1152], P(('dp', 'ctx')), may hold values from -4 to 4
- w_q: bfloat16 [1152, 1152], P(('dp', 'ctx'), 'tensor'), may hold values from -0.25 to 0.25
- b_q: bfloat16 [1152], P('tensor'), may hold values from -4 to 4
- w_k: bfloat16 [1152, 1152], P(('dp', 'ctx'), 'tensor'), may hold values from -0.25 to 0.25
- w_v: bfloat16 [1152, 1152], P(('dp', 'ctx'), 'tensor'), may hold values from -0.1875 to 0.1875
- b_v: bfloat16 [1152], P('tensor'), may hold values from -4 to 4
- w_o: bfloat16 [1152, 1152], P('tensor', ('dp', 'ctx')), may hold values from -1.5 to 1.5
- b_o: bfloat16 [1152], P(('dp', 'ctx')), may hold values from -6 to 6
- ln2_gain: bfloat16 [1152], P(('dp', 'ctx')), may hold values from 0.5 to 1.5
- ln2_bias: bfloat16 [1152], P(('dp', 'ctx')), may hold values from -4 to 4
- w_up: bfloat16 [1152, 4304], P(('dp', 'ctx'), 'tensor'), may hold values from -0.1875 to 0.1875
- b_up: bfloat16 [4304], P('tensor'), may hold values from -6 to 6
- w_down: bfloat16 [4304, 1152], P('tensor', ('dp', 'ctx')), may hold values from -0.09375 to 0.09375
- b_down: bfloat16 [1152], P(('dp', 'ctx')), may hold values from -6 to 6
Outputs:
- layer_out: bfloat16 [16, 736, 1152], P(('dp', 'tensor'), 'ctx')
- loss: float32 [], replicated
- tokens_grad: float32 [16, 736, 1152], P(('dp', 'tensor'), 'ctx')
- ln1_gain_grad: float32 [1152], P(('dp', 'ctx'))
- ln1_bias_grad: float32 [1152], P(('dp', 'ctx'))
- w_q_grad: float32 [1152, 1152], P(('dp', 'ctx'), 'tensor')
- b_q_grad: float32 [1152], P('tensor')
- w_k_grad: float32 [1152, 1152], P(('dp', 'ctx'), 'tensor')
- w_v_grad: float32 [1152, 1152], P(('dp', 'ctx'), 'tensor')
- b_v_grad: float32 [1152], P('tensor')
- w_o_grad: float32 [1152, 1152], P('tensor', ('dp', 'ctx'))
- b_o_grad: float32 [1152], P(('dp', 'ctx'))
- ln2_gain_grad: float32 [1152], P(('dp', 'ctx'))
- ln2_bias_grad: float32 [1152], P(('dp', 'ctx'))
- w_up_grad: float32 [1152, 4304], P(('dp', 'ctx'), 'tensor')
- b_up_grad: float32 [4304], P('tensor')
- w_down_grad: float32 [4304, 1152], P('tensor', ('dp', 'ctx'))
- b_down_grad: float32 [1152], P(('dp', 'ctx'))
Inputs may be any that keep to these rules, and one draw needn't show every extreme that they name: The first valid_len[s] token positions of slot s are valid and the others are not; the last slot has exactly 729 valid tokens.
All inputs are finite; a program needn't handle non-finite values.
Results may differ from a plain program's by a relative error of at most 0.014.
Values may be sent and summed in bfloat16 or wider, within the bound.
A program may use at most 192 MiB of HBM per device.

v0:
```python
import jax
import jax.numpy as jnp
from jax import lax
from jax.sharding import PartitionSpec as P

HD = 72
REAL = 729
EPSILON = 1e-06
GELU_C = 0.7978845608028654
GELU_K = 0.044715
BF = jnp.bfloat16
F32 = jnp.float32


def norm_forward(row_values, gain_vec, shift_vec):
    average = jnp.mean(row_values, axis=-1, keepdims=True)
    centred = row_values - average
    spread = jnp.mean(centred * centred, axis=-1, keepdims=True)
    inverse = lax.rsqrt(spread + EPSILON)
    unit_rows = centred * inverse
    return (unit_rows * gain_vec + shift_vec, unit_rows, inverse)


def norm_backward(upstream, unit_rows, inverse, gain_vec):
    scaled = upstream * gain_vec
    inner_sum = (
        scaled
        - jnp.mean(scaled, axis=-1, keepdims=True)
        - unit_rows * jnp.mean(scaled * unit_rows, axis=-1, keepdims=True)
    )
    return (inner_sum * inverse, jnp.sum(upstream * unit_rows, axis=0), jnp.sum(upstream, axis=0))


def gelu_tanh(values):
    return 0.5 * values * (1.0 + jnp.tanh(GELU_C * (values + GELU_K * values * values * values)))


def gelu_slope(values):
    tanh_part = jnp.tanh(GELU_C * (values + GELU_K * values * values * values))
    return 0.5 * (1.0 + tanh_part) + 0.5 * values * (1.0 - tanh_part * tanh_part) * GELU_C * (
        1.0 + 3.0 * GELU_K * values * values
    )


def swap(values, axis):
    return lax.ppermute(values, axis, [(0, 1), (1, 0)])


def tensor_gather(values):
    if lax.axis_size("tensor") == 2:
        return jnp.stack([values, swap(values, "tensor")])
    return lax.all_gather(values, "tensor", axis=0)


def tensor_reduce(partials):
    if lax.axis_size("tensor") == 2:
        return partials[0] + swap(partials[1].astype(BF), "tensor").astype(F32)
    return lax.psum_scatter(partials.astype(BF), "tensor", scatter_dimension=0).astype(F32)


def ctx_gather(values):
    if lax.axis_size("ctx") == 2:
        return jnp.concatenate([values, swap(values, "ctx")], axis=2)
    return lax.all_gather(values, "ctx", axis=2, tiled=True)


def ctx_reduce(values, half_len):
    if lax.axis_size("ctx") == 2:
        other = swap(values[:, :, half_len:].astype(BF), "ctx")
        return values[:, :, :half_len] + other.astype(F32)
    return lax.psum_scatter(values.astype(BF), "ctx", scatter_dimension=2, tiled=True).astype(F32)


def key_positions(half_len):
    n_ctx = lax.axis_size("ctx")
    local = jnp.arange(half_len * n_ctx)
    if n_ctx == 2:
        me = lax.axis_index("ctx")
        block = jnp.where(local < half_len, me, 1 - me)
        return block * half_len + local % half_len
    return local


def tree_sum(values, axes):
    for axis in axes:
        size = lax.axis_size(axis)
        if size & size - 1:
            values = jax.tree.map(lambda v: lax.psum(v, axis), values)
            continue
        step = 1
        while step < size:
            perm = [(i, i ^ step) for i in range(size)]
            values = jax.tree.map(lambda v: v + lax.ppermute(v, axis, perm), values)
            step *= 2
    return values


def on_device(
    tokens,
    teacher,
    valid_len,
    ln1_gain,
    ln1_bias,
    w_q,
    b_q,
    w_k,
    w_v,
    b_v,
    w_o,
    b_o,
    ln2_gain,
    ln2_bias,
    w_up,
    b_up,
    w_down,
    b_down,
):
    own_images, half_len, width = tokens.shape
    n_t = lax.axis_size("tensor")
    piece, head_width = w_q.shape
    local_heads = head_width // HD
    hidden_width = w_up.shape[1]
    rows = own_images * half_len
    images = n_t * own_images
    valid_count = tree_sum(jnp.sum(valid_len.astype(jnp.int32)), ("tensor", "dp")).astype(F32)
    valid_count, tokens = lax.optimization_barrier((valid_count, tokens))
    pad_hidden = -hidden_width % 128
    pad_out = -head_width % 128
    vector_rows = jnp.stack([ln1_gain, ln1_bias, b_o, ln2_gain, ln2_bias, b_down], axis=1)
    vector_slot = jnp.pad(vector_rows, ((0, 0), (0, head_width - vector_rows.shape[1])))
    attn_pack = jnp.stack([w_q, w_k, w_v, w_o.T, vector_slot])
    attn_full = lax.all_gather(attn_pack, ("dp", "ctx"), axis=1, tiled=True)
    mlp_pack = jnp.pad(jnp.stack([w_up, w_down.T]), ((0, 0), (0, 0), (0, pad_hidden)))
    mlp_full = lax.all_gather(mlp_pack, ("dp", "ctx"), axis=1, tiled=True)
    qkv_w = attn_full[:3].reshape(3, width, local_heads, HD)
    out_wt = attn_full[3]
    vectors = attn_full[4][:, :6].astype(F32)
    gain_one, shift_one, out_bias, gain_two, shift_two, down_bias = [
        vectors[:, i] for i in range(6)
    ]
    up_w, down_wt = (mlp_full[0], mlp_full[1])
    up_b = jnp.pad(b_up.astype(F32), (0, pad_hidden))
    out_per_head = out_wt.reshape(width, local_heads, HD)
    qkv_bias = jnp.stack([b_q.astype(F32), jnp.zeros((head_width,), F32), b_v.astype(F32)]).reshape(
        3, 1, local_heads, 1, HD
    )
    inputs = tokens.astype(F32).reshape(rows, width)
    normed, unit_one, inverse_one = norm_forward(inputs, gain_one, shift_one)
    normed_every_row = tensor_gather(normed.astype(BF)).reshape(images, half_len, width)
    qkv_rows = (
        jnp.einsum("pro,tojx->tpjrx", normed_every_row, qkv_w, preferred_element_type=F32)
        + qkv_bias
    ).astype(BF)
    queries, key_rows, value_rows = (qkv_rows[0], qkv_rows[1], qkv_rows[2])
    key_all = ctx_gather(key_rows)
    value_all = ctx_gather(value_rows)
    usable = key_positions(half_len) < REAL
    score_scale = HD ** (-0.5)
    raw_scores = jnp.einsum("bhqe,bhke->bhqk", queries, key_all, preferred_element_type=F32)
    scores = jnp.where(usable, raw_scores * score_scale, -1e30)
    summit = jnp.max(scores, axis=-1, keepdims=True)
    exp_total = jnp.sum(jnp.exp(scores - summit), axis=-1, keepdims=True)
    log_totals = summit + jnp.log(exp_total)
    soft_weights = jnp.exp(scores - log_totals).astype(BF)
    mixed_per_head = jnp.einsum(
        "bhqk,bhke->bhqe", soft_weights, value_all, preferred_element_type=F32
    ).astype(BF)
    attn_terms = jnp.einsum(
        "lscm,dsm->lcd", mixed_per_head, out_per_head, preferred_element_type=F32
    )
    attn_sum = tensor_reduce(attn_terms.reshape(n_t, rows, width))
    hidden = inputs + attn_sum + out_bias
    normed_two, unit_two, inverse_two = norm_forward(hidden, gain_two, shift_two)
    normed_two_all = tensor_gather(normed_two.astype(BF)).reshape(images * half_len, width)
    before = jnp.dot(normed_two_all, up_w, preferred_element_type=F32) + up_b
    active = gelu_tanh(before).astype(BF)
    mlp_terms = jnp.einsum("rf,df->rd", active, down_wt, preferred_element_type=F32)
    result = hidden + tensor_reduce(mlp_terms.reshape(n_t, rows, width)) + down_bias
    layer_out = result.astype(BF).reshape(own_images, half_len, width)
    position = lax.axis_index("ctx") * half_len + jnp.arange(half_len)
    valid_rows = (position[None, :] < valid_len[:, None]).astype(F32).reshape(rows)
    error_rows = result - teacher.astype(F32).reshape(rows, width)
    partial_value = 0.5 * jnp.sum(valid_rows * jnp.mean(error_rows * error_rows, axis=-1))
    slot_total = own_images * lax.axis_size("dp") * n_t
    factor = slot_total * (half_len * lax.axis_size("ctx")) / valid_count
    grad_out = error_rows * (valid_rows[:, None] * factor)
    grad_rows = tensor_gather(grad_out.astype(BF)).reshape(images * half_len, width)
    down_grad_t = jnp.einsum("rd,rf->df", grad_rows, active, preferred_element_type=F32)
    active_grad = jnp.einsum("rd,df->rf", grad_rows, down_wt, preferred_element_type=F32)
    before_grad = (active_grad * gelu_slope(before)).astype(BF)
    up_bias_grad = jnp.sum(before_grad[:, :hidden_width], axis=0, dtype=F32)
    up_grad = jnp.einsum("rd,rf->df", normed_two_all, before_grad, preferred_element_type=F32)
    mlp_grad_pack = jnp.concatenate([up_grad.astype(BF), down_grad_t.astype(BF)], axis=1)
    norm_two_terms = jnp.einsum("rf,df->rd", before_grad, up_w, preferred_element_type=F32)
    norm_two_grad = tensor_reduce(norm_two_terms.reshape(n_t, rows, width))
    hidden_back, gain_two_grad, shift_two_grad = norm_backward(
        norm_two_grad, unit_two, inverse_two, gain_two
    )
    hidden_grad = grad_out + hidden_back
    mlp_grad_pack, hidden_grad = lax.optimization_barrier((mlp_grad_pack, hidden_grad))
    mlp_grads = lax.psum_scatter(mlp_grad_pack, ("dp", "ctx"), scatter_dimension=0, tiled=True)
    down_bias_grad = jnp.sum(grad_out, axis=0)
    out_bias_grad = jnp.sum(hidden_grad, axis=0)
    hidden_token_rows = tensor_gather(hidden_grad.astype(BF)).reshape(images, half_len, width)
    out_grad_t = jnp.einsum(
        "lcd,lscm->dsm", hidden_token_rows, mixed_per_head, preferred_element_type=F32
    ).reshape(width, head_width)
    mixed_grad = jnp.einsum(
        "lcd,dsm->lscm", hidden_token_rows, out_per_head, preferred_element_type=F32
    ).astype(BF)
    soft_full = jnp.exp(scores - log_totals)
    soft_grad = jnp.einsum("bhqe,bhke->bhqk", mixed_grad, value_all, preferred_element_type=F32)
    value_grads = jnp.einsum(
        "bhqk,bhqe->bhke", soft_full.astype(BF), mixed_grad, preferred_element_type=F32
    )
    inner_sum = jnp.sum(soft_full * soft_grad, axis=-1, keepdims=True)
    score_grad = (soft_full * (soft_grad - inner_sum)).astype(BF)
    query_grads = (
        jnp.einsum("bhqk,bhke->bhqe", score_grad, key_all, preferred_element_type=F32) * score_scale
    )
    key_grads = (
        jnp.einsum("bhqk,bhqe->bhke", score_grad, queries, preferred_element_type=F32) * score_scale
    )
    key_reduced_precision = ctx_reduce(key_grads, half_len).astype(BF)
    value_reduced_precision = ctx_reduce(value_grads, half_len).astype(BF)
    query_reduced_precision = query_grads.astype(BF)
    query_bias_grad = jnp.sum(query_reduced_precision, axis=(0, 2), dtype=F32).reshape(head_width)
    value_bias_grad = jnp.sum(value_reduced_precision, axis=(0, 2), dtype=F32).reshape(head_width)
    qkv_grads = jnp.stack([query_reduced_precision, key_reduced_precision, value_reduced_precision])
    qkv_weight_grad = jnp.einsum(
        "okz,toaks->ztas", normed_every_row, qkv_grads, preferred_element_type=F32
    ).reshape(width, 3 * head_width)
    attn_grads = lax.psum_scatter(
        jnp.concatenate(
            [jnp.pad(out_grad_t.astype(BF), ((0, 0), (0, pad_out))), qkv_weight_grad.astype(BF)],
            axis=1,
        ),
        ("dp", "ctx"),
        scatter_dimension=0,
        tiled=True,
    )
    norm_one_terms = jnp.einsum("toaks,tzas->okz", qkv_grads, qkv_w, preferred_element_type=F32)
    norm_one_grad = tensor_reduce(norm_one_terms.reshape(n_t, rows, width))
    input_back, gain_one_grad, shift_one_grad = norm_backward(
        norm_one_grad, unit_one, inverse_one, gain_one
    )
    tokens_grad = (hidden_grad + input_back).reshape(own_images, half_len, width)
    row_sums = jnp.concatenate(
        [
            gain_one_grad,
            shift_one_grad,
            out_bias_grad,
            gain_two_grad,
            shift_two_grad,
            down_bias_grad,
            partial_value.reshape(1),
        ]
    )
    head_sums = jnp.concatenate([query_bias_grad, value_bias_grad, up_bias_grad])
    row_sums, head_sums = tree_sum((row_sums, head_sums), ("ctx", "dp"))
    row_sums = tree_sum(row_sums, ("tensor",))
    loss_value = row_sums[6 * width] / valid_count
    piece_start = lax.axis_index(("dp", "ctx")) * piece
    vector_shards = [
        lax.dynamic_slice_in_dim(row_sums, i * width + piece_start, piece) for i in range(6)
    ]
    query_bias_sum = head_sums[:head_width]
    value_bias_sum = head_sums[head_width : 2 * head_width]
    up_bias_sum = head_sums[2 * head_width :]
    attn_grads = attn_grads.astype(F32)
    mlp_grads = mlp_grads.astype(F32)
    out_cols = head_width + pad_out
    attn_grads = [
        attn_grads[:, out_cols + i * head_width : out_cols + (i + 1) * head_width] for i in range(3)
    ] + [attn_grads[:, :head_width]]
    hidden_cols = hidden_width + pad_hidden
    mlp_grads = [
        mlp_grads[:, :hidden_width],
        mlp_grads[:, hidden_cols : hidden_cols + hidden_width],
    ]
    return (
        layer_out,
        loss_value,
        tokens_grad,
        vector_shards[0],
        vector_shards[1],
        attn_grads[0],
        query_bias_sum,
        attn_grads[1],
        attn_grads[2],
        value_bias_sum,
        attn_grads[3].T,
        vector_shards[2],
        vector_shards[3],
        vector_shards[4],
        mlp_grads[0],
        up_bias_sum,
        mlp_grads[1].T,
        vector_shards[5],
    )


def solution(mesh):
    return jax.shard_map(
        on_device,
        mesh=mesh,
        in_specs=(
            P(("dp", "tensor"), "ctx", None),
            P(("dp", "tensor"), "ctx", None),
            P(("dp", "tensor")),
            P(("dp", "ctx")),
            P(("dp", "ctx")),
            P(("dp", "ctx"), "tensor"),
            P("tensor"),
            P(("dp", "ctx"), "tensor"),
            P(("dp", "ctx"), "tensor"),
            P("tensor"),
            P("tensor", ("dp", "ctx")),
            P(("dp", "ctx")),
            P(("dp", "ctx")),
            P(("dp", "ctx")),
            P(("dp", "ctx"), "tensor"),
            P("tensor"),
            P("tensor", ("dp", "ctx")),
            P(("dp", "ctx")),
        ),
        out_specs=(
            P(("dp", "tensor"), "ctx", None),
            P(),
            P(("dp", "tensor"), "ctx", None),
            P(("dp", "ctx")),
            P(("dp", "ctx")),
            P(("dp", "ctx"), "tensor"),
            P("tensor"),
            P(("dp", "ctx"), "tensor"),
            P(("dp", "ctx"), "tensor"),
            P("tensor"),
            P("tensor", ("dp", "ctx")),
            P(("dp", "ctx")),
            P(("dp", "ctx")),
            P(("dp", "ctx")),
            P(("dp", "ctx"), "tensor"),
            P("tensor"),
            P("tensor", ("dp", "ctx")),
            P(("dp", "ctx")),
        ),
        check_vma=False,
    )
```

profile of v0, /device:TPU:0, one launch (start us, length us, event | category | flops | bytes accessed | tf_op | source)
XLA Modules:
  0.0 603.0 jit_solution(12647250671530605282)
XLA Ops:
  14.6 3.1 collective-permute-start
  20.0 3.3 collective-permute-start.1
  24.3 3.4 collective-permute-start.2
  28.7 4.4 collective-permute-start.3
  34.9 49.4 %all-gather.3.cloned.1.call-done = bf16[5,1152,576]{2,1,0:T(8,128)(2,1)} async-done(((bf16[5,72,576]{2,1,0:T(8,128)(2,1)}), bf16[5,1152,576]{2,1,0:T(8,128)(2,1)}) %all-gather.3.cloned.1.call-update) | async-done | bytes 6635536 | tf_op jit(solution)/shard_map/all_gather | solution.py:132
  84.3 2.1 fusion.102
  86.5 1.8 slice_reduce_fusion
  88.6 1.5 collective-permute-start.4
  90.5 4.7 slice.162
  95.2 6.7 %copy.80 = bf16[3,1152,576]{1,2,0:T(8,128)(2,1)} copy(bf16[3,1152,576]{2,1,0:T(8,128)(2,1)} %slice.162) | data formatting | bytes 7962624 | tf_op jit(solution)/shard_map/slice | solution.py:135
  102.4 7.5 %collective-permute-done.4 = bf16[368,1152]{1,0:T(8,128)(2,1)} collective-permute-done((bf16[368,1152]{1,0:T(8,128)(2,1)S(1)}, bf16[368,1152]{1,0:T(8,128)(2,1)}, u32[]{:S(2)}, u32[]{:S(2)}) %collective-permute-start.4) | collective-permute-done | bytes 847904 | tf_op jit(solution)/shard_map/ppermute | solution.py:46
  109.8 6.1 %fusion.15 = bf16[3,2,8,368,72]{3,4,1,2,0:T(8,128)(2,1)S(1)} fusion(f32[3,8,72]{2,1,0:T(8,128)S(1)} %maximum_bitcast_fusion, bf16[3,1152,8,72,1]{1,3,4,2,0:T(8,128)(2,1)} %bitcast.218, bf16[1,368,1152]{2,1,0:T(8,128)(2,1)} %bitcast.18, bf16[1,368,1152]{2,1,0:T(8,128)(2,1)S(1)} %fusion.39), kind=kOutput, calls=%fused_computation.35 | convolution fusion | flops 2936180736 | bytes 8227584 | tf_op jit(solution)/shard_map/pro,tojx->tpjrx/dot_general | solution.py:151
  117.4 1.8 copy.84
  120.1 5.5 fusion
  125.7 4.7 exponential_reduce_fusion
  130.5 2.1 copy-done
  132.5 6.5 %fusion.57 = bf16[2,8,368,72]{2,3,1,0:T(8,128)(2,1)} fusion(f32[2,8,368,736]{3,2,1,0:T(8,128)S(1)} %get-tuple-element.68, f32[2,8,368]{2,1,0:T(8,128)S(1)} %log_add_fusion, pred[736]{0:T(1024)(128)(4,1)S(1)} %fusion.82, bf16[2,8,368,72]{2,3,0,1:T(8,128)(2,1)S(1)} %collective-permute-done.6, bf16[2,8,368,72]{2,3,0,1:T(8,128)(2,1)S(1)} %copy-done.15), kind=kOutput, calls=%fused_computation.116 | convolution fusion | flops 645183488 | bytes 19902176 | tf_op jit(solution)/shard_map/bhqk,bhke->bhqe/dot_general | solution.py:165
  139.0 2.9 convolution_bitcast_fusion
  142.0 1.5 collective-permute-start.7
  143.6 19.4 %collective-permute-done.7 = bf16[368,1152]{1,0:T(8,128)(2,1)S(1)} collective-permute-done((bf16[368,1152]{1,0:T(8,128)(2,1)S(1)}, bf16[368,1152]{1,0:T(8,128)(2,1)S(1)}, u32[]{:S(2)}, u32[]{:S(2)}) %collective-permute-start.7) | collective-permute-done | bytes 847904 | tf_op jit(solution)/shard_map/ppermute | solution.py:46
  164.1 1.5 collective-permute-start.8
  166.0 18.3 %collective-permute-done.8 = bf16[368,1152]{1,0:T(8,128)(2,1)S(1)} collective-permute-done((bf16[368,1152]{1,0:T(8,128)(2,1)S(1)}, bf16[368,1152]{1,0:T(8,128)(2,1)S(1)}, u32[]{:S(2)}, u32[]{:S(2)}) %collective-permute-start.8) | collective-permute-done | bytes 847904 | tf_op jit(solution)/shard_map/ppermute | solution.py:46
  185.7 7.6 %fusion.12 = f32[736,2176]{1,0:T(8,128)S(1)} fusion(bf16[736,1152]{1,0:T(8,128)(2,1)} %bitcast.222, bf16[2,1152,2176]{2,1,0:T(8,128)(2,1)} %all-gather.5.cloned.1.call-done), kind=kOutput, calls=%fused_computation.29 | convolution fusion | flops 3689938944 | bytes 13115392 | tf_op jit(solution)/shard_map/dot_general | solution.py:175
  193.3 5.8 fusion.13
  199.1 1.8 copy-done.21
  203.4 18.1 %collective-permute-done.9 = bf16[368,1152]{1,0:T(8,128)(2,1)} collective-permute-done((bf16[368,1152]{1,0:T(8,128)(2,1)}, bf16[368,1152]{1,0:T(8,128)(2,1)}, u32[]{:S(2)}, u32[]{:S(2)}) %collective-permute-start.9) | collective-permute-done | bytes 847904 | tf_op jit(solution)/shard_map/ppermute | solution.py:46
  221.5 3.3 multiply_reduce_fusion.1
  225.1 1.5 collective-permute-start.10
  226.6 17.0 %collective-permute-done.10 = bf16[368,1152]{1,0:T(8,128)(2,1)S(1)} collective-permute-done((bf16[368,1152]{1,0:T(8,128)(2,1)S(1)}, bf16[368,1152]{1,0:T(8,128)(2,1)S(1)}, u32[]{:S(2)}, u32[]{:S(2)}) %collective-permute-start.10) | collective-permute-done | bytes 847904 | tf_op jit(solution)/shard_map/ppermute | solution.py:46
  243.9 5.5 convolution_convert_fusion
  249.4 9.5 %fusion.9 = bf16[736,2176]{1,0:T(8,128)(2,1)S(1)} fusion(bf16[736,1152]{1,0:T(8,128)(2,1)S(1)} %bitcast.225, f32[736,2176]{1,0:T(8,128)} %copy-done.51, bf16[2,1152,2176]{2,1,0:T(8,128)(2,1)S(1)} %bitcast.240, f32[2176]{0:T(1024)S(1)} %pad_convert_fusion), kind=kOutput, calls=%fused_computation.21 | convolution fusion | flops 3721969664 | bytes 16330752 | tf_op jit(solution)/shard_map/rd,df->rf/dot_general | solution.py:189
  258.9 4.8 convolution_convert_fusion.1
  263.8 4.6 fusion.11
  268.4 1.7 copy-done.9
  272.5 4.7 pad_maximum_fusion
  277.3 11.7 %collective-permute-done.11 = bf16[368,1152]{1,0:T(8,128)(2,1)} collective-permute-done((bf16[368,1152]{1,0:T(8,128)(2,1)}, bf16[368,1152]{1,0:T(8,128)(2,1)}, u32[]{:S(2)}, u32[]{:S(2)}) %collective-permute-start.11) | collective-permute-done | bytes 847904 | tf_op jit(solution)/shard_map/ppermute | solution.py:46
  289.0 2.6 multiply_reduce_fusion.2
  291.6 4.0 multiply_add_fusion.1
  297.3 15.2 %collective-permute-done.12 = bf16[368,1152]{1,0:T(8,128)(2,1)S(1)} collective-permute-done((bf16[368,1152]{1,0:T(8,128)(2,1)S(1)}, bf16[368,1152]{1,0:T(8,128)(2,1)S(1)}, u32[]{:S(2)}, u32[]{:S(2)}) %collective-permute-start.12) | collective-permute-done | bytes 847904 | tf_op jit(solution)/shard_map/ppermute | solution.py:46
  313.9 8.4 %fusion.73 = f32[2,8,736,72]{2,3,1,0:T(8,128)S(1)} fusion(bf16[2,8,368,72]{2,3,0,1:T(8,128)(2,1)S(1)} %fusion.65, f32[2,8,368,736]{3,2,1,0:T(8,128)} %copy-done, f32[2,8,368]{2,1,0:T(8,128)S(1)} %log_add_fusion, pred[736]{0:T(1024)(128)(4,1)S(1)} %fusion.82), kind=kOutput, calls=%fused_computation.129 | convolution fusion | flops 641368064 | bytes 21597920 | tf_op jit(solution)/shard_map/bhqk,bhqe->bhke/dot_general | solution.py:213
  322.3 1.8 copy-done.19
  325.4 14.7 %multiply_reduce_fusion = (f32[2,8,368]{2,1,0:T(8,128)S(1)}, f32[2,8,368,736]{3,2,1,0:T(8,128)}) fusion(f32[2,8,368,736]{3,2,1,0:T(8,128)} %copy-done, f32[2,8,368]{2,1,0:T(8,128)S(1)} %log_add_fusion, pred[736]{0:T(1024)(128)(4,1)S(1)} %fusion.82, bf16[2,8,368,72]{2,3,0,1:T(8,128)(2,1)S(1)} %fusion.65, bf16[2,8,368,72]{2,3,0,1:T(8,128)(2,1)S(1)} %copy-done.30, ...), kind=kOutput, calls=%fused_computation.1 | convolution fusion | flops 649087232 | bytes 37260000 | tf_op jit(solution)/shard_map/bhqe,bhke->bhqk/dot_general | solution.py:212
  340.0 12.9 %multiply_convert_fusion = bf16[2,8,368,736]{3,2,1,0:T(8,128)(2,1)S(1)} fusion(f32[2,8,368,736]{3,2,1,0:T(8,128)} %get-tuple-element.70, f32[2,8,368,736]{3,2,1,0:T(8,128)} %copy-done, f32[2,8,368]{2,1,0:T(8,128)S(1)} %get-tuple-element.69, f32[2,8,368]{2,1,0:T(8,128)S(1)} %log_add_fusion, pred[736]{0:T(1024)(128)(4,1)S(1)} %fusion.82), kind=kLoop, calls=%fused_computation | loop fusion | flops 26001408 | bytes 43383520 | tf_op jit(solution)/shard_map/convert_element_type | solution.py:217
  353.0 1.5 convolution_multiply_fusion
  354.5 2.0 copy-done.3
  356.5 3.8 fusion.14
  360.3 2.8 copy.91
  364.0 7.5 %convert_reduce_fusion.3 = (f32[8,72]{1,0:T(8,128)}, bf16[2,8,368,72]{2,3,1,0:T(8,128)(2,1)S(1)}) fusion(bf16[2,8,368,736]{3,2,1,0:T(8,128)(2,1)} %copy-done.3, bf16[2,8,368,72]{2,3,0,1:T(8,128)(2,1)} %collective-permute-done.5, bf16[2,8,368,72]{2,3,0,1:T(8,128)(2,1)} %get-tuple-element.51), kind=kOutput, calls=%fused_computation.58 | convolution fusion | flops 629120448 | bytes 11213056 | tf_op jit(solution)/shard_map/bhqk,bhke->bhqe/dot_general | solution.py:219
  371.6 2.5 convert_reduce_fusion.2
  374.3 6.6 %bitcast_convert_fusion = bf16[1152,3,8,72]{0,3,2,1:T(8,128)(2,1)} fusion(bf16[1,368,1152]{2,1,0:T(8,128)(2,1)} %bitcast.18, bf16[1,368,1152]{2,1,0:T(8,128)(2,1)S(1)} %copy-done.32, bf16[1,2,8,368,72]{3,4,2,1,0:T(8,128)(2,1)S(1)} %get-tuple-element.48, bf16[1,2,8,368,72]{3,4,2,1,0:T(8,128)(2,1)S(1)} %fusion.70, bf16[1,2,8,368,72]{3,4,2,1,0:T(8,128)(2,1)S(1)} %bitcast.243), kind=kOutput, calls=%fused_computation.14 | convolution fusion | flops 2943258624 | bytes 8220672 | tf_op jit(solution)/shard_map/okz,toaks->ztas/dot_general | solution.py:230
  381.0 6.6 %copy.93 = bf16[1152,1728]{1,0:T(8,128)(2,1)} copy(bf16[1152,1728]{0,1:T(8,128)(2,1)} %bitcast.220) | data formatting | bytes 7962624 | tf_op jit(solution)/shard_map/convert_element_type | solution.py:235
  387.5 5.3 fusion.10
  394.4 6.3 %convolution_bitcast_fusion.1 = f32[2,368,1152]{2,1,0:T(8,128)S(1)} fusion(bf16[3,1152,8,72,1]{1,3,2,4,0:T(8,128)(2,1)} %bitcast.219, bf16[1,2,8,368,72]{3,4,2,1,0:T(8,128)(2,1)S(1)} %copy-done.28, bf16[1,2,8,368,72]{3,4,2,1,0:T(8,128)(2,1)S(1)} %copy-done.26, bf16[1,2,8,368,72]{3,4,2,1,0:T(8,128)(2,1)} %bitcast.244), kind=kOutput, calls=%fused_computation.32 | convolution fusion | flops 2932789248 | bytes 9916416 | tf_op jit(solution)/shard_map/toaks,tzas->okz/dot_general | solution.py:242
  400.6 1.8 copy-done.11
  406.1 18.2 %collective-permute-done.15 = bf16[368,1152]{1,0:T(8,128)(2,1)S(1)} collective-permute-done((bf16[368,1152]{1,0:T(8,128)(2,1)}, bf16[368,1152]{1,0:T(8,128)(2,1)S(1)}, u32[]{:S(2)}, u32[]{:S(2)}) %collective-permute-start.15) | collective-permute-done | bytes 847904 | tf_op jit(solution)/shard_map/ppermute | solution.py:46
  424.3 2.4 fusion.29
  426.7 2.0 fusion.33
  430.9 3.7 collective-permute-done.17
  438.5 2.5 collective-permute-start.19
  442.4 4.3 collective-permute-done.23
  447.2 4.9 collective-permute-done.24
  457.9 17.1 %reduce-scatter.7.cloned.1.call-done = bf16[72,2368]{1,0:T(8,128)(2,1)} async-done(((bf16[1152,2368]{1,0:T(8,128)(2,1)}), bf16[72,2368]{1,0:T(8,128)(2,1)}) %reduce-scatter.7.cloned.1.call-update) | async-done | bytes 341008
  476.6 1.8 fusion.103
  478.5 113.4 %reduce-scatter.5.cloned.1.call-done = bf16[72,4352]{1,0:T(8,128)(2,1)} async-done(((bf16[1152,4352]{1,0:T(8,128)(2,1)}), bf16[72,4352]{1,0:T(8,128)(2,1)}) %reduce-scatter.5.cloned.1.call-update) | async-done | bytes 626704 | tf_op jit(solution)/shard_map/reduce_scatter | solution.py:201
  (230 shorter events, 50.0 us)
Async XLA Ops:
  7.2 6.4 %copy-start.33 = (bf16[2152,72]{0,1:T(8,128)(2,1)S(1)}, bf16[2152,72]{0,1:T(8,128)(2,1)}, u32[]{:S(2)}) copy-start(bf16[2152,72]{0,1:T(8,128)(2,1)} %param.34) | copy-start | bytes 929668
  7.2 27.1 %copy-start.1 = (bf16[1,368,1152]{2,1,0:T(8,128)(2,1)S(1)}, bf16[1,368,1152]{2,1,0:T(8,128)(2,1)}, u32[]{:S(2)}) copy-start(bf16[1,368,1152]{2,1,0:T(8,128)(2,1)} %param.18) | copy-start | bytes 2543620
  7.2 77.1 %all-gather.3.cloned.1.call-start = ((), (), s32[]{:S(2)}) async-start(), calls=%async_computation.2 | async-start | bytes 7833600 | tf_op jit(solution)/shard_map/all_gather | solution.py:132
  13.6 172.1 %all-gather.5.cloned.1.call-start = ((), (), s32[]{:S(2)}) async-start(), calls=%async_computation.3 | async-start | bytes 10653696 | tf_op jit(solution)/shard_map/all_gather | solution.py:134
  14.5 460.4 %reduce-scatter.7.cloned.1.call-start = ((), (), s32[]{:S(2)}) async-start(), calls=%async_computation.5 | async-start | bytes 5953536
  14.6 4.9 collective-permute-start
  20.0 3.7 collective-permute-start.1
  24.3 3.8 collective-permute-start.2
  28.7 5.0 collective-permute-start.3
  34.5 67.4 %copy-start.37 = (f32[368]{0:T(512)}, f32[368]{0:T(512)S(1)}, u32[]{:S(2)}) copy-start(f32[368]{0:T(512)S(1)} %broadcast_multiply_fusion.5) | copy-start | bytes 4420
  34.9 67.0 %copy-start.39 = (f32[368]{0:T(512)}, f32[368]{0:T(512)S(1)}, u32[]{:S(2)}) copy-start(f32[368]{0:T(512)S(1)} %add_rsqrt_fusion.1) | copy-start | bytes 4420
  88.2 13.7 %copy-start.35 = (f32[1152]{0:T(1024)}, f32[1152]{0:T(1024)S(1)}, u32[]{:S(2)}) copy-start(f32[1152]{0:T(1024)S(1)} %get-tuple-element.41) | copy-start | bytes 13828
  88.6 21.2 %collective-permute-start.4 = (bf16[368,1152]{1,0:T(8,128)(2,1)S(1)}, bf16[368,1152]{1,0:T(8,128)(2,1)}, u32[]{:S(2)}, u32[]{:S(2)}) collective-permute-start(bf16[368,1152]{1,0:T(8,128)(2,1)S(1)} %fusion.27), channel_id=1, source_target_pairs={{0,1},{1,0},{2,3},{3,2},{4,5},{5,4},{6,7},{7,6},{8,9},{9,8},{10,11... | collective-permute-start | bytes 2543624 | tf_op jit(solution)/shard_map/ppermute | solution.py:46
  102.4 13.5 %copy-start.31 = (bf16[1,368,1152]{2,1,0:T(8,128)(2,1)}, bf16[1,368,1152]{2,1,0:T(8,128)(2,1)S(1)}, u32[]{:S(2)}) copy-start(bf16[1,368,1152]{2,1,0:T(8,128)(2,1)S(1)} %fusion.39) | copy-start | bytes 2543620
  117.4 8.3 %copy-start.13 = (bf16[2,8,368,72]{2,3,0,1:T(8,128)(2,1)}, bf16[2,8,368,72]{2,3,0,1:T(8,128)(2,1)S(1)}, u32[]{:S(2)}) copy-start(bf16[2,8,368,72]{2,3,0,1:T(8,128)(2,1)S(1)} %get-tuple-element.49) | copy-start | bytes 2543620
  117.4 2.8 collective-permute-start.5
  119.2 11.3 %collective-permute-start.6 = (bf16[2,8,368,72]{2,3,0,1:T(8,128)(2,1)}, bf16[2,8,368,72]{2,3,0,1:T(8,128)(2,1)S(1)}, u32[]{:S(2)}, u32[]{:S(2)}) collective-permute-start(bf16[2,8,368,72]{2,3,0,1:T(8,128)(2,1)} %get-tuple-element.50), channel_id=1, source_target_pairs={{0,2},{2,0},{1,3},{3,1},{4,6},{6,4},{5,7},{7,5},{8,10},{10,8},{9,1... | collective-permute-start | bytes 2543624 | tf_op jit(solution)/shard_map/ppermute | solution.py:46
  125.7 6.9 %copy-start = (f32[2,8,368,736]{3,2,1,0:T(8,128)}, f32[2,8,368,736]{3,2,1,0:T(8,128)S(1)}, u32[]{:S(2)}) copy-start(f32[2,8,368,736]{3,2,1,0:T(8,128)S(1)} %get-tuple-element.68) | copy-start | bytes 52002820
  125.7 6.9 %copy-start.15 = (bf16[2,8,368,72]{2,3,0,1:T(8,128)(2,1)S(1)}, bf16[2,8,368,72]{2,3,0,1:T(8,128)(2,1)}, u32[]{:S(2)}) copy-start(bf16[2,8,368,72]{2,3,0,1:T(8,128)(2,1)} %get-tuple-element.50) | copy-start | bytes 2543620
  130.4 8.6 %copy-start.23 = (bf16[1,1152,576]{1,2,0:T(8,128)(2,1)S(1)}, bf16[1,1152,576]{1,2,0:T(8,128)(2,1)}, u32[]{:S(2)}) copy-start(bf16[1,1152,576]{1,2,0:T(8,128)(2,1)} %copy.84) | copy-start | bytes 3981316
  132.5 6.5 %copy-start.29 = (bf16[2,8,368,72]{2,3,0,1:T(8,128)(2,1)}, bf16[2,8,368,72]{2,3,0,1:T(8,128)(2,1)S(1)}, u32[]{:S(2)}) copy-start(bf16[2,8,368,72]{2,3,0,1:T(8,128)(2,1)S(1)} %collective-permute-done.6) | copy-start | bytes 2543620
  142.0 21.0 %collective-permute-start.7 = (bf16[368,1152]{1,0:T(8,128)(2,1)S(1)}, bf16[368,1152]{1,0:T(8,128)(2,1)S(1)}, u32[]{:S(2)}, u32[]{:S(2)}) collective-permute-start(bf16[368,1152]{1,0:T(8,128)(2,1)S(1)} %fusion.71), channel_id=1, source_target_pairs={{0,1},{1,0},{2,3},{3,2},{4,5},{5,4},{6,7},{7,6},{8,9},{9,8},{10,11... | collective-permute-start | bytes 2543624 | tf_op jit(solution)/shard_map/ppermute | solution.py:46
  164.1 20.2 %collective-permute-start.8 = (bf16[368,1152]{1,0:T(8,128)(2,1)S(1)}, bf16[368,1152]{1,0:T(8,128)(2,1)S(1)}, u32[]{:S(2)}, u32[]{:S(2)}) collective-permute-start(bf16[368,1152]{1,0:T(8,128)(2,1)S(1)} %add_convert_fusion.1), channel_id=1, source_target_pairs={{0,1},{1,0},{2,3},{3,2},{4,5},{5,4},{6,7},{7,6},{8,9},{9,8},{10,11... | collective-permute-start | bytes 2543624 | tf_op jit(solution)/shard_map/ppermute | solution.py:46
  185.7 7.6 %copy-start.48 = (bf16[2,1152,2176]{2,1,0:T(8,128)(2,1)S(1)}, bf16[2,1152,2176]{2,1,0:T(8,128)(2,1)}, u32[]{:S(2)}) copy-start(bf16[2,1152,2176]{2,1,0:T(8,128)(2,1)} %all-gather.5.cloned.1.call-done) | copy-start | bytes 30081028
  193.3 28.2 %copy-start.7 = (bf16[1,368,1152]{2,1,0:T(8,128)(2,1)S(1)}, bf16[1,368,1152]{2,1,0:T(8,128)(2,1)}, u32[]{:S(2)}) copy-start(bf16[1,368,1152]{2,1,0:T(8,128)(2,1)} %param.19) | copy-start | bytes 2543620
  201.9 19.6 %collective-permute-start.9 = (bf16[368,1152]{1,0:T(8,128)(2,1)}, bf16[368,1152]{1,0:T(8,128)(2,1)}, u32[]{:S(2)}, u32[]{:S(2)}) collective-permute-start(bf16[368,1152]{1,0:T(8,128)(2,1)} %slice.279), channel_id=1, source_target_pairs={{0,1},{1,0},{2,3},{3,2},{4,5},{5,4},{6,7},{7,6},{8,9},{9,8},{10,11... | collective-permute-start | bytes 2543624 | tf_op jit(solution)/shard_map/ppermute | solution.py:46
  221.5 22.3 %slice-start.3 = ((s8[6406144]{0:T(1024)(128)(4,1)}), s8[4194304]{0:T(1024)(128)(4,1)S(1)}, s32[]{:S(2)}) async-start(s8[6406144]{0:T(1024)(128)(4,1)} %bitcast.245), calls=%async_computation.9 | async-start | bytes 8388608
  221.5 22.3 %slice-start.4 = ((s8[6406144]{0:T(1024)(128)(4,1)}), s8[2211840]{0:T(1024)(128)(4,1)S(1)}, s32[]{:S(2)}) async-start(s8[6406144]{0:T(1024)(128)(4,1)} %bitcast.245), calls=%async_computation.10 | async-start | bytes 4423680
  224.8 19.0 %copy-start.6 = (f32[368,1152]{1,0:T(8,128)}, f32[368,1152]{1,0:T(8,128)S(1)}, u32[]{:S(2)}) copy-start(f32[368,1152]{1,0:T(8,128)S(1)} %get-tuple-element.42) | copy-start | bytes 5087236
  225.1 18.5 %collective-permute-start.10 = (bf16[368,1152]{1,0:T(8,128)(2,1)S(1)}, bf16[368,1152]{1,0:T(8,128)(2,1)S(1)}, u32[]{:S(2)}, u32[]{:S(2)}) collective-permute-start(bf16[368,1152]{1,0:T(8,128)(2,1)S(1)} %multiply_convert_fusion.3), channel_id=1, source_target_pairs={{0,1},{1,0},{2,3},{3,2},{4,5},{5,4},{6,7},{7,6},{8,9},{9,8},{10,11... | collective-permute-start | bytes 2543624 | tf_op jit(solution)/shard_map/ppermute | solution.py:46
  249.4 9.5 %copy-start.22 = (bf16[2,368,1152]{2,1,0:T(8,128)(2,1)S(1)}, bf16[2,368,1152]{2,1,0:T(8,128)(2,1)}, u32[]{:S(2)}) copy-start(bf16[2,368,1152]{2,1,0:T(8,128)(2,1)} %pad_maximum_fusion.5) | copy-start | bytes 5087236
  271.1 17.9 %collective-permute-start.11 = (bf16[368,1152]{1,0:T(8,128)(2,1)}, bf16[368,1152]{1,0:T(8,128)(2,1)}, u32[]{:S(2)}, u32[]{:S(2)}) collective-permute-start(bf16[368,1152]{1,0:T(8,128)(2,1)} %slice.278), channel_id=1, source_target_pairs={{0,1},{1,0},{2,3},{3,2},{4,5},{5,4},{6,7},{7,6},{8,9},{9,8},{10,11... | collective-permute-start | bytes 2543624 | tf_op jit(solution)/shard_map/ppermute | solution.py:46
  277.3 14.3 %copy-start.10 = (f32[736,1152]{1,0:T(8,128)S(1)}, f32[736,1152]{1,0:T(8,128)}, u32[]{:S(2)}) copy-start(f32[736,1152]{1,0:T(8,128)} %copy-done.9) | copy-start | bytes 10174468
  295.6 16.9 %copy-start.24 = (bf16[1,1152,576]{1,2,0:T(8,128)(2,1)S(1)}, bf16[1,1152,576]{1,2,0:T(8,128)(2,1)}, u32[]{:S(2)}) copy-start(bf16[1,1152,576]{1,2,0:T(8,128)(2,1)} %copy.84) | copy-start | bytes 3981316
  295.7 16.8 %collective-permute-start.12 = (bf16[368,1152]{1,0:T(8,128)(2,1)S(1)}, bf16[368,1152]{1,0:T(8,128)(2,1)S(1)}, u32[]{:S(2)}, u32[]{:S(2)}) collective-permute-start(bf16[368,1152]{1,0:T(8,128)(2,1)S(1)} %convert_element_type.165), channel_id=1, source_target_pairs={{0,1},{1,0},{2,3},{3,2},{4,5},{5,4},{6,7},{7,6},{8,9},{9,8},{10,11... | collective-permute-start | bytes 2543624 | tf_op jit(solution)/shard_map/ppermute | solution.py:46
  313.9 11.5 %copy-start.30 = (bf16[2,8,368,72]{2,3,0,1:T(8,128)(2,1)S(1)}, bf16[2,8,368,72]{2,3,0,1:T(8,128)(2,1)}, u32[]{:S(2)}) copy-start(bf16[2,8,368,72]{2,3,0,1:T(8,128)(2,1)} %copy-done.29) | copy-start | bytes 2543620
  325.4 46.2 %collective-permute-start.14 = (bf16[2,8,368,72]{2,3,1,0:T(8,128)(2,1)}, bf16[2,8,368,72]{2,3,1,0:T(8,128)(2,1)}, u32[]{:S(2)}, u32[]{:S(2)}) collective-permute-start(bf16[2,8,368,72]{2,3,1,0:T(8,128)(2,1)} %slice.276), channel_id=1, source_target_pairs={{0,2},{2,0},{1,3},{3,1},{4,6},{6,4},{5,7},{7,5},{8,10},{10,8},{9,1... | collective-permute-start | bytes 2543624 | tf_op jit(solution)/shard_map/ppermute | solution.py:46
  340.0 12.9 %copy-start.14 = (bf16[2,8,368,72]{2,3,0,1:T(8,128)(2,1)S(1)}, bf16[2,8,368,72]{2,3,0,1:T(8,128)(2,1)}, u32[]{:S(2)}) copy-start(bf16[2,8,368,72]{2,3,0,1:T(8,128)(2,1)} %copy-done.13) | copy-start | bytes 2543620
  363.5 8.1 %copy-start.20 = (f32[2,8,736,72]{2,3,1,0:T(8,128)S(1)}, f32[2,8,736,72]{2,3,1,0:T(8,128)}, u32[]{:S(2)}) copy-start(f32[2,8,736,72]{2,3,1,0:T(8,128)} %copy-done.19) | copy-start | bytes 10174468
  363.5 10.6 %collective-permute-start.13 = (bf16[2,8,368,72]{2,3,1,0:T(8,128)(2,1)S(1)}, bf16[2,8,368,72]{2,3,1,0:T(8,128)(2,1)S(1)}, u32[]{:S(2)}, u32[]{:S(2)}) collective-permute-start(bf16[2,8,368,72]{2,3,1,0:T(8,128)(2,1)S(1)} %slice.277), channel_id=1, source_target_pairs={{0,2},{2,0},{1,3},{3,1},{4,6},{6,4},{5,7},{7,5},{8,10},{10,8},{9,1... | collective-permute-start | bytes 2543624 | tf_op jit(solution)/shard_map/ppermute | solution.py:46
  374.1 6.9 %copy-start.27 = (bf16[1,2,8,368,72]{3,4,2,1,0:T(8,128)(2,1)}, bf16[1,2,8,368,72]{3,4,2,1,0:T(8,128)(2,1)S(1)}, u32[]{:S(2)}) copy-start(bf16[1,2,8,368,72]{3,4,2,1,0:T(8,128)(2,1)S(1)} %get-tuple-element.48) | copy-start | bytes 2543620
  374.3 6.7 %copy-start.25 = (bf16[1,2,8,368,72]{3,4,2,1,0:T(8,128)(2,1)}, bf16[1,2,8,368,72]{3,4,2,1,0:T(8,128)(2,1)S(1)}, u32[]{:S(2)}) copy-start(bf16[1,2,8,368,72]{3,4,2,1,0:T(8,128)(2,1)S(1)} %fusion.70) | copy-start | bytes 2543620
  381.0 6.6 %copy-start.8 = (bf16[1152,576]{1,0:T(8,128)(2,1)S(1)}, bf16[1152,576]{1,0:T(8,128)(2,1)}, u32[]{:S(2)}) copy-start(bf16[1152,576]{1,0:T(8,128)(2,1)} %copy.91) | copy-start | bytes 3981316
  392.9 199.0 %reduce-scatter.5.cloned.1.call-start = ((), (), s32[]{:S(2)}) async-start(), calls=%async_computation.4 | async-start | bytes 10653696 | tf_op jit(solution)/shard_map/reduce_scatter | solution.py:201
  394.3 10.5 %copy-start.43 = (f32[368]{0:T(512)S(1)}, f32[368]{0:T(512)}, u32[]{:S(2)}) copy-start(f32[368]{0:T(512)} %get-tuple-element.34) | copy-start | bytes 4420
  394.3 29.9 %copy-start.2 = (bf16[1,368,1152]{2,1,0:T(8,128)(2,1)S(1)}, bf16[1,368,1152]{2,1,0:T(8,128)(2,1)}, u32[]{:S(2)}) copy-start(bf16[1,368,1152]{2,1,0:T(8,128)(2,1)} %param.18) | copy-start | bytes 2543620
  394.3 29.9 %copy-start.36 = (f32[1152]{0:T(1024)S(1)}, f32[1152]{0:T(1024)}, u32[]{:S(2)}) copy-start(f32[1152]{0:T(1024)} %copy-done.35) | copy-start | bytes 13828
  394.3 29.9 %copy-start.38 = (f32[368]{0:T(512)S(1)}, f32[368]{0:T(512)}, u32[]{:S(2)}) copy-start(f32[368]{0:T(512)} %copy-done.37) | copy-start | bytes 4420
  394.3 29.9 %copy-start.40 = (f32[368]{0:T(512)S(1)}, f32[368]{0:T(512)}, u32[]{:S(2)}) copy-start(f32[368]{0:T(512)} %copy-done.39) | copy-start | bytes 4420
  402.4 24.3 %copy-start.5 = (f32[368,1152]{1,0:T(8,128)S(1)}, f32[368,1152]{1,0:T(8,128)}, u32[]{:S(2)}) copy-start(f32[368,1152]{1,0:T(8,128)} %copy-done.4) | copy-start | bytes 5087236
  403.4 20.9 %collective-permute-start.15 = (bf16[368,1152]{1,0:T(8,128)(2,1)}, bf16[368,1152]{1,0:T(8,128)(2,1)S(1)}, u32[]{:S(2)}, u32[]{:S(2)}) collective-permute-start(bf16[368,1152]{1,0:T(8,128)(2,1)} %fusion.72), channel_id=1, source_target_pairs={{0,1},{1,0},{2,3},{3,2},{4,5},{5,4},{6,7},{7,6},{8,9},{9,8},{10,11... | collective-permute-start | bytes 2543624 | tf_op jit(solution)/shard_map/ppermute | solution.py:46
  406.1 20.6 %copy-start.12 = (f32[2,368,1152]{2,1,0:T(8,128)S(1)}, f32[2,368,1152]{2,1,0:T(8,128)}, u32[]{:S(2)}) copy-start(f32[2,368,1152]{2,1,0:T(8,128)} %copy-done.11) | copy-start | bytes 10174468
  426.7 9.0 %copy-start.17 = (bf16[736,2176]{1,0:T(8,128)(2,1)S(1)}, bf16[736,2176]{1,0:T(8,128)(2,1)}, u32[]{:S(2)}) copy-start(bf16[736,2176]{1,0:T(8,128)(2,1)} %copy-done.16) | copy-start | bytes 9609220
  428.7 7.5 %copy-start.45 = (f32[8,72]{1,0:T(8,128)S(1)}, f32[8,72]{1,0:T(8,128)}, u32[]{:S(2)}) copy-start(f32[8,72]{1,0:T(8,128)} %get-tuple-element.71) | copy-start | bytes 6916
  428.7 7.6 %copy-start.42 = (f32[8,72]{1,0:T(8,128)S(1)}, f32[8,72]{1,0:T(8,128)}, u32[]{:S(2)}) copy-start(f32[8,72]{1,0:T(8,128)} %get-tuple-element.47) | copy-start | bytes 6916
  428.8 1.3 collective-permute-start.16
  430.1 4.6 collective-permute-start.17
  434.7 3.9 collective-permute-start.18
  436.5 1.2 collective-permute-start.21
  437.7 3.7 collective-permute-start.22
  438.5 13.6 %collective-permute-start.19 = (f32[6913]{0:T(1024)S(1)}, f32[6913]{0:T(1024)S(1)}, u32[]{:S(2)}, u32[]{:S(2)}) collective-permute-start(f32[6913]{0:T(1024)S(1)} %add.281), channel_id=1, source_target_pairs={{0,16},{4,20},{8,24},{12,28},{16,0},{20,4},{24,8},{28,12},{1,17},{... | collective-permute-start | bytes 82964 | tf_op jit(solution)/shard_map/ppermute | solution.py:93
  441.4 5.2 collective-permute-start.23
  446.7 5.4 collective-permute-start.24
  452.1 3.9 collective-permute-start.20
  (22 other events, 69.6 us)
Sparse Core Ops, SparseCore 0:
  13.7 70.5 all-gather.2
  87.1 83.4 all-gather.4
  393.0 81.8 reduce-scatter.6
  478.9 112.8 reduce-scatter.4
where the time goes:
time: 608 us; the launch traced here: 603 us
  waiting for transfers between devices  326 us (54%)
  matrix products  109 us (18%)
  local copies, waits for them, and re-layouts  58.2 us (10%)
  other arithmetic  54 us (9%)
  starting transfers between devices  35.7 us (6%)
  between operations  20.7 us (3%)
    ppermute x12, waiting for transfers between devices, swap(): return lax.ppermute(values, axis, [(0, 1), (1, 0)])  126 us
    reduce_scatter x1, waiting for transfers between devices, on_device(): lax.psum_scatter(mlp_grad_pack, ('dp', 'ctx'), scatter_dimension=0, tiled...  113 us
    all_gather x1, waiting for transfers between devices, on_device(): attn_full = lax.all_gather(attn_pack, ('dp', 'ctx'), axis=1, tiled=True)  49.4 us
    ppermute x13, starting transfers between devices, tree_sum(): values = jax.tree.map(lambda v: v + lax.ppermute(v, axis, perm), values)  22.5 us
    ppermute x13, waiting for transfers between devices, tree_sum(): values = jax.tree.map(lambda v: v + lax.ppermute(v, axis, perm), values)  19.3 us
    unnamed x5, waiting for transfers between devices  17.6 us
    unnamed x128, local copies, waits for them, and re-layouts  16.5 us
    dot_general x1, matrix products, on_device(): jnp.einsum('bhqe,bhke->bhqk', mixed_grad, value_all, preferred_element_ty...  14.7 us
  transfers between devices with their start and end apart: 29, of which 23 were waited for; matrix products, arithmetic and copies ran while one was open for 20% of the time, Pallas kernels for 0%

commit v1 on v0

--- a/solution.py
+++ b/solution.py
@@ -10,6 +10,27 @@
 GELU_K = 0.044715
 BF = jnp.bfloat16
 F32 = jnp.float32
+
+
+def collect(value, axis, dim):
+    peers, position, width = (lax.axis_size(axis), lax.axis_index(axis), value.shape[dim])
+    forward = [(i, (i + 1) % peers) for i in range(peers)]
+    downward = [(i, (i - 1) % peers) for i in range(peers)]
+    out = jnp.zeros((*value.shape[:dim], peers * width, *value.shape[dim + 1 :]), value.dtype)
+    out = lax.dynamic_update_slice_in_dim(out, value, position * width, axis=dim)
+    from_left = from_right = value
+    half = peers // 2
+    for hop in range(1, half + 1):
+        from_left = lax.ppermute(from_left, axis, forward)
+        out = lax.dynamic_update_slice_in_dim(
+            out, from_left, (position - hop) % peers * width, axis=dim
+        )
+        if hop < peers - half:
+            from_right = lax.ppermute(from_right, axis, downward)
+            out = lax.dynamic_update_slice_in_dim(
+                out, from_right, (position + hop) % peers * width, axis=dim
+            )
+    return out
 
 
 def norm_forward(row_values, gain_vec, shift_vec):
@@ -129,7 +150,7 @@
     vector_rows = jnp.stack([ln1_gain, ln1_bias, b_o, ln2_gain, ln2_bias, b_down], axis=1)
     vector_slot = jnp.pad(vector_rows, ((0, 0), (0, head_width - vector_rows.shape[1])))
     attn_pack = jnp.stack([w_q, w_k, w_v, w_o.T, vector_slot])
-    attn_full = lax.all_gather(attn_pack, ("dp", "ctx"), axis=1, tiled=True)
+    attn_full = collect(attn_pack, ("dp", "ctx"), 1)
     mlp_pack = jnp.pad(jnp.stack([w_up, w_down.T]), ((0, 0), (0, 0), (0, pad_hidden)))
     mlp_full = lax.all_gather(mlp_pack, ("dp", "ctx"), axis=1, tiled=True)
     qkv_w = attn_full[:3].reshape(3, width, local_heads, HD)

time: 608 us -> 896 us (1.47); the launches traced: 603 us -> 880 us
  local copies, waits for them, and re-layouts: 58.2 us -> 274 us
  starting transfers between devices: 35.7 us -> 77.6 us
  waiting for transfers between devices: 326 us -> 347 us
    dynamic_update_slice x0 -> x16, local copies, waits for them, and re-layouts: none -> 214 us  [the longest x8 108 us: collect(): lax.dynamic_update_slice_in_dim(out, from_left, (position - hop) % peers...]
    ppermute x0 -> x15, waiting for transfers between devices: none -> 57 us  [the longest x7 41 us: collect(): from_right = lax.ppermute(from_right, axis, downward)]
    all_gather x1 -> x0, waiting for transfers between devices: 49.4 us -> none  [on_device(): attn_full = lax.all_gather(attn_pack, ('dp', 'ctx'), axis=1, tiled=True)]
    ppermute x0 -> x15, starting transfers between devices: none -> 45.4 us  [the longest x7 28.3 us: collect(): from_right = lax.ppermute(from_right, axis, downward)]
    ppermute x12, waiting for transfers between devices: 126 us -> 138 us  [swap(): return lax.ppermute(values, axis, [(0, 1), (1, 0)])]
    ppermute x0 -> x15, local copies, waits for them, and re-layouts: none -> 10.5 us  [the longest x7 5.59 us: collect(): from_right = lax.ppermute(from_right, axis, downward)]
    slice x2 -> x1, local copies, waits for them, and re-layouts: 11.4 us -> 2.43 us  [on_device(): qkv_w = attn_full[:3].reshape(3, width, local_heads, HD)]
  transfers between devices with their start and end apart: 29 -> 43, of which waited for: 23 -> 32; matrix products, arithmetic and copies ran while one was open for 20% -> 38% of each run, Pallas kernels for 0% -> 0%
where the time goes in v1:
time: 896 us; the launch traced here: 880 us
  waiting for transfers between devices  347 us (39%)
  local copies, waits for them, and re-layouts  274 us (31%)
  matrix products  106 us (12%)
  starting transfers between devices  77.6 us (9%)
  other arithmetic  54.9 us (6%)
  between operations  20.5 us (2%)
    ppermute x12, waiting for transfers between devices, swap(): return lax.ppermute(values, axis, [(0, 1), (1, 0)])  138 us
    reduce_scatter x1, waiting for transfers between devices, on_device(): lax.psum_scatter(mlp_grad_pack, ('dp', 'ctx'), scatter_dimension=0, tiled...  114 us
    dynamic_update_slice x8, local copies, waits for them, and re-layouts, collect(): lax.dynamic_update_slice_in_dim(out, from_left, (position - hop) % peers...  108 us
    dynamic_update_slice x7, local copies, waits for them, and re-layouts, collect(): lax.dynamic_update_slice_in_dim(out, from_right, (position + hop) % peers...  94.7 us
    ppermute x7, waiting for transfers between devices, collect(): from_right = lax.ppermute(from_right, axis, downward)  41 us
    ppermute x7, starting transfers between devices, collect(): from_right = lax.ppermute(from_right, axis, downward)  28.3 us
    ppermute x13, starting transfers between devices, tree_sum(): values = jax.tree.map(lambda v: v + lax.ppermute(v, axis, perm), values)  21.3 us
    ppermute x13, waiting for transfers between devices, tree_sum(): values = jax.tree.map(lambda v: v + lax.ppermute(v, axis, perm), values)  21.2 us
  transfers between devices with their start and end apart: 43, of which 32 were waited for; matrix products, arithmetic and copies ran while one was open for 38% of the time, Pallas kernels for 0%

profile of v1, /device:TPU:0, one launch (start us, length us, event | category | flops | bytes accessed | tf_op | source)
XLA Modules:
  0.0 880.1 jit_solution(6072038745289855896)
XLA Ops:
  15.2 5.0 collective-permute-start.5
  20.3 6.3 collective-permute-done.4
  26.5 4.8 collective-permute-start.6
  33.8 4.6 collective-permute-start.7
  38.4 8.7 collective-permute-done.6
  47.0 5.8 collective-permute-done.7
  52.8 4.6 collective-permute-start.9
  57.8 15.5 %collective-permute-done.9 = bf16[5,72,576]{2,1,0:T(8,128)(2,1)S(1)} collective-permute-done((bf16[5,72,576]{2,1,0:T(8,128)(2,1)S(1)}, bf16[5,72,576]{2,1,0:T(8,128)(2,1)S(1)}, u32[]{:S(2)}, u32[]{:S(2)}) %collective-permute-start.9) | collective-permute-done | bytes 414752 | tf_op jit(solution)/shard_map/ppermute | solution.py:29
  73.3 4.6 collective-permute-start.11
  78.2 12.7 %collective-permute-done.11 = bf16[5,72,576]{2,1,0:T(8,128)(2,1)S(1)} collective-permute-done((bf16[5,72,576]{2,1,0:T(8,128)(2,1)S(1)}, bf16[5,72,576]{2,1,0:T(8,128)(2,1)S(1)}, u32[]{:S(2)}, u32[]{:S(2)}) %collective-permute-start.11) | collective-permute-done | bytes 414752 | tf_op jit(solution)/shard_map/ppermute | solution.py:29
  90.9 4.6 collective-permute-start.13
  95.9 4.5 collective-permute-start.14
  100.4 4.5 collective-permute-done.13
  104.9 4.8 collective-permute-start.15
  109.8 6.8 collective-permute-start.16
  121.4 11.8 %dynamic_update_slice.48 = bf16[5,1152,576]{1,2,0:T(8,128)(2,1)} dynamic-update-slice(bf16[5,1152,576]{1,2,0:T(8,128)(2,1)} %broadcast_in_dim.21, bf16[5,72,576]{1,2,0:T(8,128)(2,1)S(1)} %bitcast_dynamic-update-slice_fusion.1, s32[]{:T(128)} %constant.149.clone.1, s32[]{:T(128)S(6)} %select_n.145, s32[]{:T(128)} %constant.149.clone.1) | dynamic-update-slice | bytes 829444 | tf_op jit(solution)/shard_map/dynamic_update_slice | solution.py:20
  133.8 5.6 collective-permute-start.1
  145.1 4.6 collective-permute-start.3
  152.2 13.1 %dynamic_update_slice.49 = bf16[5,1152,576]{1,2,0:T(8,128)(2,1)} dynamic-update-slice(bf16[5,1152,576]{1,2,0:T(8,128)(2,1)} %dynamic_update_slice.48, bf16[5,72,576]{1,2,0:T(8,128)(2,1)S(1)} %copy.59, s32[]{:T(128)} %constant.149.clone.1, s32[]{:T(128)S(6)} %select_n.147, s32[]{:T(128)} %constant.149.clone.1) | dynamic-update-slice | bytes 829444 | tf_op jit(solution)/shard_map/dynamic_update_slice | solution.py:25
  165.6 13.5 %dynamic_update_slice.50 = bf16[5,1152,576]{1,2,0:T(8,128)(2,1)} dynamic-update-slice(bf16[5,1152,576]{1,2,0:T(8,128)(2,1)} %dynamic_update_slice.49, bf16[5,72,576]{1,2,0:T(8,128)(2,1)S(1)} %copy.61, s32[]{:T(128)} %constant.149.clone.1, s32[]{:T(128)S(6)} %select_n.149, s32[]{:T(128)} %constant.149.clone.1) | dynamic-update-slice | bytes 829444 | tf_op jit(solution)/shard_map/dynamic_update_slice | solution.py:30
  179.5 13.6 %dynamic_update_slice.51 = bf16[5,1152,576]{1,2,0:T(8,128)(2,1)} dynamic-update-slice(bf16[5,1152,576]{1,2,0:T(8,128)(2,1)} %dynamic_update_slice.50, bf16[5,72,576]{1,2,0:T(8,128)(2,1)S(1)} %copy.62, s32[]{:T(128)} %constant.149.clone.1, s32[]{:T(128)S(6)} %select_n.151, s32[]{:T(128)} %constant.149.clone.1) | dynamic-update-slice | bytes 829444 | tf_op jit(solution)/shard_map/dynamic_update_slice | solution.py:25
  193.4 13.6 %dynamic_update_slice.52 = bf16[5,1152,576]{1,2,0:T(8,128)(2,1)} dynamic-update-slice(bf16[5,1152,576]{1,2,0:T(8,128)(2,1)} %dynamic_update_slice.51, bf16[5,72,576]{1,2,0:T(8,128)(2,1)S(1)} %copy.63, s32[]{:T(128)} %constant.149.clone.1, s32[]{:T(128)S(6)} %select_n.153, s32[]{:T(128)} %constant.149.clone.1) | dynamic-update-slice | bytes 829444 | tf_op jit(solution)/shard_map/dynamic_update_slice | solution.py:30
  207.4 13.6 %dynamic_update_slice.53 = bf16[5,1152,576]{1,2,0:T(8,128)(2,1)} dynamic-update-slice(bf16[5,1152,576]{1,2,0:T(8,128)(2,1)} %dynamic_update_slice.52, bf16[5,72,576]{1,2,0:T(8,128)(2,1)S(1)} %copy.64, s32[]{:T(128)} %constant.149.clone.1, s32[]{:T(128)S(6)} %select_n.155, s32[]{:T(128)} %constant.149.clone.1) | dynamic-update-slice | bytes 829444 | tf_op jit(solution)/shard_map/dynamic_update_slice | solution.py:25
  221.3 13.6 %dynamic_update_slice.54 = bf16[5,1152,576]{1,2,0:T(8,128)(2,1)} dynamic-update-slice(bf16[5,1152,576]{1,2,0:T(8,128)(2,1)} %dynamic_update_slice.53, bf16[5,72,576]{1,2,0:T(8,128)(2,1)S(1)} %copy.65, s32[]{:T(128)} %constant.149.clone.1, s32[]{:T(128)S(6)} %select_n.157, s32[]{:T(128)} %constant.149.clone.1) | dynamic-update-slice | bytes 829444 | tf_op jit(solution)/shard_map/dynamic_update_slice | solution.py:30
  235.2 13.5 %dynamic_update_slice.55 = bf16[5,1152,576]{1,2,0:T(8,128)(2,1)} dynamic-update-slice(bf16[5,1152,576]{1,2,0:T(8,128)(2,1)} %dynamic_update_slice.54, bf16[5,72,576]{1,2,0:T(8,128)(2,1)S(1)} %copy.66, s32[]{:T(128)} %constant.149.clone.1, s32[]{:T(128)S(6)} %select_n.159, s32[]{:T(128)} %constant.149.clone.1) | dynamic-update-slice | bytes 829444 | tf_op jit(solution)/shard_map/dynamic_update_slice | solution.py:25
  249.1 13.5 %dynamic_update_slice.56 = bf16[5,1152,576]{1,2,0:T(8,128)(2,1)} dynamic-update-slice(bf16[5,1152,576]{1,2,0:T(8,128)(2,1)} %dynamic_update_slice.55, bf16[5,72,576]{1,2,0:T(8,128)(2,1)S(1)} %copy.67, s32[]{:T(128)} %constant.149.clone.1, s32[]{:T(128)S(6)} %select_n.161, s32[]{:T(128)} %constant.149.clone.1) | dynamic-update-slice | bytes 829444 | tf_op jit(solution)/shard_map/dynamic_update_slice | solution.py:30
  263.0 13.5 %dynamic_update_slice.57 = bf16[5,1152,576]{1,2,0:T(8,128)(2,1)} dynamic-update-slice(bf16[5,1152,576]{1,2,0:T(8,128)(2,1)} %dynamic_update_slice.56, bf16[5,72,576]{1,2,0:T(8,128)(2,1)S(1)} %copy.68, s32[]{:T(128)} %constant.149.clone.1, s32[]{:T(128)S(6)} %select_n.163, s32[]{:T(128)} %constant.149.clone.1) | dynamic-update-slice | bytes 829444 | tf_op jit(solution)/shard_map/dynamic_update_slice | solution.py:25
  277.9 13.5 %dynamic_update_slice.58 = bf16[5,1152,576]{1,2,0:T(8,128)(2,1)} dynamic-update-slice(bf16[5,1152,576]{1,2,0:T(8,128)(2,1)} %dynamic_update_slice.57, bf16[5,72,576]{1,2,0:T(8,128)(2,1)S(1)} %copy.69, s32[]{:T(128)} %constant.149.clone.1, s32[]{:T(128)S(6)} %select_n.165, s32[]{:T(128)} %constant.149.clone.1) | dynamic-update-slice | bytes 829444 | tf_op jit(solution)/shard_map/dynamic_update_slice | solution.py:30
  292.9 13.5 %dynamic_update_slice.59 = bf16[5,1152,576]{1,2,0:T(8,128)(2,1)} dynamic-update-slice(bf16[5,1152,576]{1,2,0:T(8,128)(2,1)} %dynamic_update_slice.58, bf16[5,72,576]{1,2,0:T(8,128)(2,1)S(1)} %copy.70, s32[]{:T(128)} %constant.149.clone.1, s32[]{:T(128)S(6)} %select_n.167, s32[]{:T(128)} %constant.149.clone.1) | dynamic-update-slice | bytes 829444 | tf_op jit(solution)/shard_map/dynamic_update_slice | solution.py:25
  307.7 13.5 %dynamic_update_slice.60 = bf16[5,1152,576]{1,2,0:T(8,128)(2,1)} dynamic-update-slice(bf16[5,1152,576]{1,2,0:T(8,128)(2,1)} %dynamic_update_slice.59, bf16[5,72,576]{1,2,0:T(8,128)(2,1)S(1)} %copy.71, s32[]{:T(128)} %constant.149.clone.1, s32[]{:T(128)S(6)} %select_n.169, s32[]{:T(128)} %constant.149.clone.1) | dynamic-update-slice | bytes 829444 | tf_op jit(solution)/shard_map/dynamic_update_slice | solution.py:30
  321.6 13.5 %dynamic_update_slice.61 = bf16[5,1152,576]{1,2,0:T(8,128)(2,1)} dynamic-update-slice(bf16[5,1152,576]{1,2,0:T(8,128)(2,1)} %dynamic_update_slice.60, bf16[5,72,576]{1,2,0:T(8,128)(2,1)S(1)} %copy.72, s32[]{:T(128)} %constant.149.clone.1, s32[]{:T(128)S(6)} %select_n.171, s32[]{:T(128)} %constant.149.clone.1) | dynamic-update-slice | bytes 829444 | tf_op jit(solution)/shard_map/dynamic_update_slice | solution.py:25
  336.5 13.5 %dynamic_update_slice.62 = bf16[5,1152,576]{1,2,0:T(8,128)(2,1)} dynamic-update-slice(bf16[5,1152,576]{1,2,0:T(8,128)(2,1)} %dynamic_update_slice.61, bf16[5,72,576]{1,2,0:T(8,128)(2,1)S(1)} %copy.73, s32[]{:T(128)} %constant.149.clone.1, s32[]{:T(128)S(6)} %select_n.173, s32[]{:T(128)} %constant.149.clone.1) | dynamic-update-slice | bytes 829444 | tf_op jit(solution)/shard_map/dynamic_update_slice | solution.py:30
  351.4 13.6 %dynamic_update_slice.63 = bf16[5,1152,576]{1,2,0:T(8,128)(2,1)} dynamic-update-slice(bf16[5,1152,576]{1,2,0:T(8,128)(2,1)} %dynamic_update_slice.62, bf16[5,72,576]{1,2,0:T(8,128)(2,1)S(1)} %copy.74, s32[]{:T(128)} %constant.149.clone.1, s32[]{:T(128)S(6)} %select_n.175, s32[]{:T(128)} %constant.149.clone.1) | dynamic-update-slice | bytes 829444 | tf_op jit(solution)/shard_map/dynamic_update_slice | solution.py:25
  372.9 16.1 %collective-permute-done.19 = bf16[368,1152]{1,0:T(8,128)(2,1)S(1)} collective-permute-done((bf16[368,1152]{1,0:T(8,128)(2,1)S(1)}, bf16[368,1152]{1,0:T(8,128)(2,1)S(1)}, u32[]{:S(2)}, u32[]{:S(2)}) %collective-permute-start.19) | collective-permute-done | bytes 847904 | tf_op jit(solution)/shard_map/ppermute | solution.py:67
  397.9 5.5 fusion
  403.4 4.7 exponential_reduce_fusion
  409.9 6.3 fusion.57
  420.4 19.7 %collective-permute-done.22 = bf16[368,1152]{1,0:T(8,128)(2,1)S(1)} collective-permute-done((bf16[368,1152]{1,0:T(8,128)(2,1)S(1)}, bf16[368,1152]{1,0:T(8,128)(2,1)S(1)}, u32[]{:S(2)}, u32[]{:S(2)}) %collective-permute-start.22) | collective-permute-done | bytes 847904 | tf_op jit(solution)/shard_map/ppermute | solution.py:67
  442.8 18.5 %collective-permute-done.23 = bf16[368,1152]{1,0:T(8,128)(2,1)S(1)} collective-permute-done((bf16[368,1152]{1,0:T(8,128)(2,1)S(1)}, bf16[368,1152]{1,0:T(8,128)(2,1)S(1)}, u32[]{:S(2)}, u32[]{:S(2)}) %collective-permute-start.23) | collective-permute-done | bytes 847904 | tf_op jit(solution)/shard_map/ppermute | solution.py:67
  462.7 7.6 fusion.12
  470.3 5.8 fusion.13
  480.1 18.3 %collective-permute-done.24 = bf16[368,1152]{1,0:T(8,128)(2,1)} collective-permute-done((bf16[368,1152]{1,0:T(8,128)(2,1)}, bf16[368,1152]{1,0:T(8,128)(2,1)}, u32[]{:S(2)}, u32[]{:S(2)}) %collective-permute-start.24) | collective-permute-done | bytes 847904 | tf_op jit(solution)/shard_map/ppermute | solution.py:67
  503.5 17.2 %collective-permute-done.25 = bf16[368,1152]{1,0:T(8,128)(2,1)S(1)} collective-permute-done((bf16[368,1152]{1,0:T(8,128)(2,1)S(1)}, bf16[368,1152]{1,0:T(8,128)(2,1)S(1)}, u32[]{:S(2)}, u32[]{:S(2)}) %collective-permute-start.25) | collective-permute-done | bytes 847904 | tf_op jit(solution)/shard_map/ppermute | solution.py:67
  520.9 5.5 convolution_convert_fusion
  526.5 9.5 %fusion.9 = bf16[736,2176]{1,0:T(8,128)(2,1)S(1)} fusion(bf16[736,1152]{1,0:T(8,128)(2,1)S(1)} %bitcast.226, f32[736,2176]{1,0:T(8,128)} %copy-done.63, bf16[2,1152,2176]{2,1,0:T(8,128)(2,1)S(1)} %bitcast.241, f32[2176]{0:T(1024)S(1)} %pad_convert_fusion), kind=kOutput, calls=%fused_computation.21 | convolution fusion | flops 3721969664 | bytes 16330752 | tf_op jit(solution)/shard_map/rd,df->rf/dot_general | solution.py:210
  536.0 4.8 convolution_convert_fusion.1
  540.8 4.6 fusion.11
  549.3 4.6 pad_maximum_fusion
  553.9 12.0 %collective-permute-done.26 = bf16[368,1152]{1,0:T(8,128)(2,1)} collective-permute-done((bf16[368,1152]{1,0:T(8,128)(2,1)}, bf16[368,1152]{1,0:T(8,128)(2,1)}, u32[]{:S(2)}, u32[]{:S(2)}) %collective-permute-start.26) | collective-permute-done | bytes 847904 | tf_op jit(solution)/shard_map/ppermute | solution.py:67
  568.5 4.0 multiply_add_fusion.1
  574.0 15.3 %collective-permute-done.27 = bf16[368,1152]{1,0:T(8,128)(2,1)S(1)} collective-permute-done((bf16[368,1152]{1,0:T(8,128)(2,1)S(1)}, bf16[368,1152]{1,0:T(8,128)(2,1)S(1)}, u32[]{:S(2)}, u32[]{:S(2)}) %collective-permute-start.27) | collective-permute-done | bytes 847904 | tf_op jit(solution)/shard_map/ppermute | solution.py:67
  590.7 8.4 fusion.73
  602.2 14.6 %multiply_reduce_fusion = (f32[2,8,368]{2,1,0:T(8,128)S(1)}, f32[2,8,368,736]{3,2,1,0:T(8,128)}) fusion(f32[2,8,368,736]{3,2,1,0:T(8,128)} %copy-done, f32[2,8,368]{2,1,0:T(8,128)S(1)} %log_add_fusion, pred[736]{0:T(1024)(128)(4,1)S(1)} %fusion.82, bf16[2,8,368,72]{2,3,0,1:T(8,128)(2,1)S(1)} %fusion.65, bf16[2,8,368,72]{2,3,0,1:T(8,128)(2,1)S(1)} %copy-done.30, ...), kind=kOutput, calls=%fused_computation.1 | convolution fusion | flops 649087232 | bytes 37260000 | tf_op jit(solution)/shard_map/bhqe,bhke->bhqk/dot_general | solution.py:233
  616.8 12.9 %multiply_convert_fusion = bf16[2,8,368,736]{3,2,1,0:T(8,128)(2,1)S(1)} fusion(f32[2,8,368,736]{3,2,1,0:T(8,128)} %get-tuple-element.70, f32[2,8,368,736]{3,2,1,0:T(8,128)} %copy-done, f32[2,8,368]{2,1,0:T(8,128)S(1)} %get-tuple-element.69, f32[2,8,368]{2,1,0:T(8,128)S(1)} %log_add_fusion, pred[736]{0:T(1024)(128)(4,1)S(1)} %fusion.82), kind=kLoop, calls=%fused_computation | loop fusion | flops 26001408 | bytes 43383520 | tf_op jit(solution)/shard_map/convert_element_type | solution.py:238
  640.9 8.4 convert_reduce_fusion.3
  651.9 5.2 bitcast_convert_fusion
  657.1 6.5 copy.88
  663.6 5.3 fusion.10
  670.4 6.3 convolution_bitcast_fusion.1
  682.0 18.4 %collective-permute-done.30 = bf16[368,1152]{1,0:T(8,128)(2,1)S(1)} collective-permute-done((bf16[368,1152]{1,0:T(8,128)(2,1)}, bf16[368,1152]{1,0:T(8,128)(2,1)S(1)}, u32[]{:S(2)}, u32[]{:S(2)}) %collective-permute-start.30) | collective-permute-done | bytes 847904 | tf_op jit(solution)/shard_map/ppermute | solution.py:67
  718.6 5.6 collective-permute-done.38
  724.1 5.6 collective-permute-done.39
  735.5 16.5 %reduce-scatter.7.cloned.1.call-done = bf16[72,2368]{1,0:T(8,128)(2,1)} async-done(((bf16[1152,2368]{1,0:T(8,128)(2,1)}), bf16[72,2368]{1,0:T(8,128)(2,1)}) %reduce-scatter.7.cloned.1.call-update) | async-done | bytes 341008
  755.6 113.6 %reduce-scatter.5.cloned.1.call-done = bf16[72,4352]{1,0:T(8,128)(2,1)} async-done(((bf16[1152,4352]{1,0:T(8,128)(2,1)}), bf16[72,4352]{1,0:T(8,128)(2,1)}) %reduce-scatter.5.cloned.1.call-update) | async-done | bytes 626704 | tf_op jit(solution)/shard_map/reduce_scatter | solution.py:222
  (311 shorter events, 129.7 us)
Async XLA Ops:
  7.2 455.5 %all-gather.2.cloned.1.call-start = ((), (), s32[]{:S(2)}) async-start(), calls=%async_computation.2 | async-start | bytes 10653696 | tf_op jit(solution)/shard_map/all_gather | solution.py:155
  9.2 742.9 %reduce-scatter.7.cloned.1.call-start = ((), (), s32[]{:S(2)}) async-start(), calls=%async_computation.4 | async-start | bytes 5953536
  14.7 11.8 %collective-permute-start.4 = (bf16[5,72,576]{2,1,0:T(8,128)(2,1)S(1)}, bf16[5,72,576]{2,1,0:T(8,128)(2,1)S(1)}, u32[]{:S(2)}, u32[]{:S(2)}) collective-permute-start(bf16[5,72,576]{2,1,0:T(8,128)(2,1)S(1)} %copy.58), channel_id=1, source_target_pairs={{0,2},{2,4},{4,6},{6,8},{8,10},{10,12},{12,14},{14,16},{16,18},{18... | collective-permute-start | bytes 1244168 | tf_op jit(solution)/shard_map/ppermute | solution.py:24
  15.2 18.5 %collective-permute-start.5 = (bf16[5,72,576]{2,1,0:T(8,128)(2,1)S(1)}, bf16[5,72,576]{2,1,0:T(8,128)(2,1)S(1)}, u32[]{:S(2)}, u32[]{:S(2)}) collective-permute-start(bf16[5,72,576]{2,1,0:T(8,128)(2,1)S(1)} %copy.58), channel_id=1, source_target_pairs={{0,30},{2,0},{4,2},{6,4},{8,6},{10,8},{12,10},{14,12},{16,14},{18,... | collective-permute-start | bytes 1244168 | tf_op jit(solution)/shard_map/ppermute | solution.py:29
  26.5 20.5 %collective-permute-start.6 = (bf16[5,72,576]{2,1,0:T(8,128)(2,1)S(1)}, bf16[5,72,576]{2,1,0:T(8,128)(2,1)S(1)}, u32[]{:S(2)}, u32[]{:S(2)}) collective-permute-start(bf16[5,72,576]{2,1,0:T(8,128)(2,1)S(1)} %collective-permute-done.4), channel_id=1, source_target_pairs={{0,2},{2,4},{4,6},{6,8},{8,10},{10,12},{12,14},{14,16},{16,18},{18... | collective-permute-start | bytes 1244168 | tf_op jit(solution)/shard_map/ppermute | solution.py:24
  33.8 19.1 %collective-permute-start.7 = (bf16[5,72,576]{2,1,0:T(8,128)(2,1)S(1)}, bf16[5,72,576]{2,1,0:T(8,128)(2,1)S(1)}, u32[]{:S(2)}, u32[]{:S(2)}) collective-permute-start(bf16[5,72,576]{2,1,0:T(8,128)(2,1)S(1)} %collective-permute-done.5), channel_id=1, source_target_pairs={{0,30},{2,0},{4,2},{6,4},{8,6},{10,8},{12,10},{14,12},{16,14},{18,... | collective-permute-start | bytes 1244168 | tf_op jit(solution)/shard_map/ppermute | solution.py:29
  47.0 10.7 %collective-permute-start.8 = (bf16[5,72,576]{2,1,0:T(8,128)(2,1)S(1)}, bf16[5,72,576]{2,1,0:T(8,128)(2,1)S(1)}, u32[]{:S(2)}, u32[]{:S(2)}) collective-permute-start(bf16[5,72,576]{2,1,0:T(8,128)(2,1)S(1)} %collective-permute-done.6), channel_id=1, source_target_pairs={{0,2},{2,4},{4,6},{6,8},{8,10},{10,12},{12,14},{14,16},{16,18},{18... | collective-permute-start | bytes 1244168 | tf_op jit(solution)/shard_map/ppermute | solution.py:24
  52.8 56.8 %copy-start.33 = (bf16[5,72,576]{2,1,0:T(8,128)(2,1)}, bf16[5,72,576]{2,1,0:T(8,128)(2,1)S(1)}, u32[]{:S(2)}) copy-start(bf16[5,72,576]{2,1,0:T(8,128)(2,1)S(1)} %collective-permute-done.7) | copy-start | bytes 1244164
  52.8 20.4 %collective-permute-start.9 = (bf16[5,72,576]{2,1,0:T(8,128)(2,1)S(1)}, bf16[5,72,576]{2,1,0:T(8,128)(2,1)S(1)}, u32[]{:S(2)}, u32[]{:S(2)}) collective-permute-start(bf16[5,72,576]{2,1,0:T(8,128)(2,1)S(1)} %collective-permute-done.7), channel_id=1, source_target_pairs={{0,30},{2,0},{4,2},{6,4},{8,6},{10,8},{12,10},{14,12},{16,14},{18,... | collective-permute-start | bytes 1244168 | tf_op jit(solution)/shard_map/ppermute | solution.py:29
  57.8 52.0 %copy-start.35 = (bf16[5,72,576]{2,1,0:T(8,128)(2,1)}, bf16[5,72,576]{2,1,0:T(8,128)(2,1)S(1)}, u32[]{:S(2)}) copy-start(bf16[5,72,576]{2,1,0:T(8,128)(2,1)S(1)} %collective-permute-done.8) | copy-start | bytes 1244164
  57.8 20.4 %collective-permute-start.10 = (bf16[5,72,576]{2,1,0:T(8,128)(2,1)S(1)}, bf16[5,72,576]{2,1,0:T(8,128)(2,1)S(1)}, u32[]{:S(2)}, u32[]{:S(2)}) collective-permute-start(bf16[5,72,576]{2,1,0:T(8,128)(2,1)S(1)} %collective-permute-done.8), channel_id=1, source_target_pairs={{0,2},{2,4},{4,6},{6,8},{8,10},{10,12},{12,14},{14,16},{16,18},{18... | collective-permute-start | bytes 1244168 | tf_op jit(solution)/shard_map/ppermute | solution.py:24
  73.3 43.3 %copy-start.37 = (bf16[5,72,576]{2,1,0:T(8,128)(2,1)}, bf16[5,72,576]{2,1,0:T(8,128)(2,1)S(1)}, u32[]{:S(2)}) copy-start(bf16[5,72,576]{2,1,0:T(8,128)(2,1)S(1)} %collective-permute-done.9) | copy-start | bytes 1244164
  73.3 17.6 %collective-permute-start.11 = (bf16[5,72,576]{2,1,0:T(8,128)(2,1)S(1)}, bf16[5,72,576]{2,1,0:T(8,128)(2,1)S(1)}, u32[]{:S(2)}, u32[]{:S(2)}) collective-permute-start(bf16[5,72,576]{2,1,0:T(8,128)(2,1)S(1)} %collective-permute-done.9), channel_id=1, source_target_pairs={{0,30},{2,0},{4,2},{6,4},{8,6},{10,8},{12,10},{14,12},{16,14},{18,... | collective-permute-start | bytes 1244168 | tf_op jit(solution)/shard_map/ppermute | solution.py:29
  78.2 38.4 %copy-start.39 = (bf16[5,72,576]{2,1,0:T(8,128)(2,1)}, bf16[5,72,576]{2,1,0:T(8,128)(2,1)S(1)}, u32[]{:S(2)}) copy-start(bf16[5,72,576]{2,1,0:T(8,128)(2,1)S(1)} %collective-permute-done.10) | copy-start | bytes 1244164
  78.2 17.7 %collective-permute-start.12 = (bf16[5,72,576]{2,1,0:T(8,128)(2,1)S(1)}, bf16[5,72,576]{2,1,0:T(8,128)(2,1)S(1)}, u32[]{:S(2)}, u32[]{:S(2)}) collective-permute-start(bf16[5,72,576]{2,1,0:T(8,128)(2,1)S(1)} %collective-permute-done.10), channel_id=1, source_target_pairs={{0,2},{2,4},{4,6},{6,8},{8,10},{10,12},{12,14},{14,16},{16,18},{18... | collective-permute-start | bytes 1244168 | tf_op jit(solution)/shard_map/ppermute | solution.py:24
  90.9 26.4 %copy-start.41 = (bf16[5,72,576]{2,1,0:T(8,128)(2,1)}, bf16[5,72,576]{2,1,0:T(8,128)(2,1)S(1)}, u32[]{:S(2)}) copy-start(bf16[5,72,576]{2,1,0:T(8,128)(2,1)S(1)} %collective-permute-done.11) | copy-start | bytes 1244164
  90.9 14.0 %collective-permute-start.13 = (bf16[5,72,576]{2,1,0:T(8,128)(2,1)S(1)}, bf16[5,72,576]{2,1,0:T(8,128)(2,1)}, u32[]{:S(2)}, u32[]{:S(2)}) collective-permute-start(bf16[5,72,576]{2,1,0:T(8,128)(2,1)S(1)} %collective-permute-done.11), channel_id=1, source_target_pairs={{0,30},{2,0},{4,2},{6,4},{8,6},{10,8},{12,10},{14,12},{16,14},{18,... | collective-permute-start | bytes 1244168 | tf_op jit(solution)/shard_map/ppermute | solution.py:29
  95.9 13.9 %collective-permute-start.14 = (bf16[5,72,576]{2,1,0:T(8,128)(2,1)S(1)}, bf16[5,72,576]{2,1,0:T(8,128)(2,1)}, u32[]{:S(2)}, u32[]{:S(2)}) collective-permute-start(bf16[5,72,576]{2,1,0:T(8,128)(2,1)S(1)} %collective-permute-done.12), channel_id=1, source_target_pairs={{0,2},{2,4},{4,6},{6,8},{8,10},{10,12},{12,14},{14,16},{16,18},{18... | collective-permute-start | bytes 1244168 | tf_op jit(solution)/shard_map/ppermute | solution.py:24
  104.9 46.0 %collective-permute-start.15 = (bf16[5,72,576]{2,1,0:T(8,128)(2,1)}, bf16[5,72,576]{2,1,0:T(8,128)(2,1)}, u32[]{:S(2)}, u32[]{:S(2)}) collective-permute-start(bf16[5,72,576]{2,1,0:T(8,128)(2,1)} %collective-permute-done.13), channel_id=1, source_target_pairs={{0,30},{2,0},{4,2},{6,4},{8,6},{10,8},{12,10},{14,12},{16,14},{18,... | collective-permute-start | bytes 1244168 | tf_op jit(solution)/shard_map/ppermute | solution.py:29
  109.8 41.2 %collective-permute-start.16 = (bf16[5,72,576]{2,1,0:T(8,128)(2,1)}, bf16[5,72,576]{2,1,0:T(8,128)(2,1)S(1)}, u32[]{:S(2)}, u32[]{:S(2)}) collective-permute-start(bf16[5,72,576]{2,1,0:T(8,128)(2,1)} %collective-permute-done.14), channel_id=1, source_target_pairs={{0,2},{2,4},{4,6},{6,8},{8,10},{10,12},{12,14},{14,16},{16,18},{18... | collective-permute-start | bytes 1244168 | tf_op jit(solution)/shard_map/ppermute | solution.py:24
  116.6 16.6 %collective-permute-start = (s32[]{:T(128)}, s32[]{:T(128)}, u32[]{:S(2)}, u32[]{:S(2)}) collective-permute-start(s32[]{:T(128)} %bitcast), channel_id=1, source_target_pairs={{0,1},{1,0},{2,3},{3,2},{4,5},{5,4},{6,7},{7,6},{8,9},{9,8},{10,11... | collective-permute-start | bytes 20 | tf_op jit(solution)/shard_map/ppermute | solution.py:114
  118.0 32.7 %copy-start.1 = (bf16[1,368,1152]{2,1,0:T(8,128)(2,1)S(1)}, bf16[1,368,1152]{2,1,0:T(8,128)(2,1)}, u32[]{:S(2)}) copy-start(bf16[1,368,1152]{2,1,0:T(8,128)(2,1)} %param.18) | copy-start | bytes 2543620
  133.8 6.0 collective-permute-start.1
  140.3 4.3 collective-permute-start.2
  145.1 5.0 collective-permute-start.3
  150.9 184.2 %collective-permute-start.17 = (bf16[5,72,576]{2,1,0:T(8,128)(2,1)}, bf16[5,72,576]{2,1,0:T(8,128)(2,1)}, u32[]{:S(2)}, u32[]{:S(2)}) collective-permute-start(bf16[5,72,576]{2,1,0:T(8,128)(2,1)} %collective-permute-done.15), channel_id=1, source_target_pairs={{0,30},{2,0},{4,2},{6,4},{8,6},{10,8},{12,10},{14,12},{16,14},{18,... | collective-permute-start | bytes 1244168 | tf_op jit(solution)/shard_map/ppermute | solution.py:29
  150.9 199.1 %collective-permute-start.18 = (bf16[5,72,576]{2,1,0:T(8,128)(2,1)S(1)}, bf16[5,72,576]{2,1,0:T(8,128)(2,1)}, u32[]{:S(2)}, u32[]{:S(2)}) collective-permute-start(bf16[5,72,576]{2,1,0:T(8,128)(2,1)S(1)} %collective-permute-done.16), channel_id=1, source_target_pairs={{0,2},{2,4},{4,6},{6,8},{8,10},{10,12},{12,14},{14,16},{16,18},{18... | collective-permute-start | bytes 1244168 | tf_op jit(solution)/shard_map/ppermute | solution.py:24
  151.4 221.0 %copy-start.47 = (f32[368]{0:T(512)}, f32[368]{0:T(512)S(1)}, u32[]{:S(2)}) copy-start(f32[368]{0:T(512)S(1)} %broadcast_multiply_fusion.5) | copy-start | bytes 4420
  151.8 220.7 %copy-start.49 = (f32[368]{0:T(512)}, f32[368]{0:T(512)S(1)}, u32[]{:S(2)}) copy-start(f32[368]{0:T(512)S(1)} %add_rsqrt_fusion.1) | copy-start | bytes 4420
  152.2 40.9 %copy-start.34 = (bf16[5,72,576]{2,1,0:T(8,128)(2,1)S(1)}, bf16[5,72,576]{2,1,0:T(8,128)(2,1)}, u32[]{:S(2)}) copy-start(bf16[5,72,576]{2,1,0:T(8,128)(2,1)} %copy-done.33) | copy-start | bytes 1244164
  165.6 41.4 %copy-start.36 = (bf16[5,72,576]{2,1,0:T(8,128)(2,1)S(1)}, bf16[5,72,576]{2,1,0:T(8,128)(2,1)}, u32[]{:S(2)}) copy-start(bf16[5,72,576]{2,1,0:T(8,128)(2,1)} %copy-done.35) | copy-start | bytes 1244164
  179.5 41.4 %copy-start.38 = (bf16[5,72,576]{2,1,0:T(8,128)(2,1)S(1)}, bf16[5,72,576]{2,1,0:T(8,128)(2,1)}, u32[]{:S(2)}) copy-start(bf16[5,72,576]{2,1,0:T(8,128)(2,1)} %copy-done.37) | copy-start | bytes 1244164
  193.4 41.4 %copy-start.40 = (bf16[5,72,576]{2,1,0:T(8,128)(2,1)S(1)}, bf16[5,72,576]{2,1,0:T(8,128)(2,1)}, u32[]{:S(2)}) copy-start(bf16[5,72,576]{2,1,0:T(8,128)(2,1)} %copy-done.39) | copy-start | bytes 1244164
  207.4 41.4 %copy-start.42 = (bf16[5,72,576]{2,1,0:T(8,128)(2,1)S(1)}, bf16[5,72,576]{2,1,0:T(8,128)(2,1)}, u32[]{:S(2)}) copy-start(bf16[5,72,576]{2,1,0:T(8,128)(2,1)} %copy-done.41) | copy-start | bytes 1244164
  221.3 41.4 %copy-start.44 = (bf16[5,72,576]{2,1,0:T(8,128)(2,1)S(1)}, bf16[5,72,576]{2,1,0:T(8,128)(2,1)}, u32[]{:S(2)}) copy-start(bf16[5,72,576]{2,1,0:T(8,128)(2,1)} %copy-done.43) | copy-start | bytes 1244164
  368.5 20.5 %collective-permute-start.19 = (bf16[368,1152]{1,0:T(8,128)(2,1)S(1)}, bf16[368,1152]{1,0:T(8,128)(2,1)S(1)}, u32[]{:S(2)}, u32[]{:S(2)}) collective-permute-start(bf16[368,1152]{1,0:T(8,128)(2,1)S(1)} %fusion.27), channel_id=1, source_target_pairs={{0,1},{1,0},{2,3},{3,2},{4,5},{5,4},{6,7},{7,6},{8,9},{9,8},{10,11... | collective-permute-start | bytes 2543624 | tf_op jit(solution)/shard_map/ppermute | solution.py:67
  395.1 2.8 collective-permute-start.20
  395.1 13.1 %collective-permute-start.21 = (bf16[2,8,368,72]{2,3,0,1:T(8,128)(2,1)S(1)}, bf16[2,8,368,72]{2,3,0,1:T(8,128)(2,1)S(1)}, u32[]{:S(2)}, u32[]{:S(2)}) collective-permute-start(bf16[2,8,368,72]{2,3,0,1:T(8,128)(2,1)S(1)} %get-tuple-element.50), channel_id=1, source_target_pairs={{0,2},{2,0},{1,3},{3,1},{4,6},{6,4},{5,7},{7,5},{8,10},{10,8},{9,1... | collective-permute-start | bytes 2543624 | tf_op jit(solution)/shard_map/ppermute | solution.py:67
  419.1 21.0 %collective-permute-start.22 = (bf16[368,1152]{1,0:T(8,128)(2,1)S(1)}, bf16[368,1152]{1,0:T(8,128)(2,1)S(1)}, u32[]{:S(2)}, u32[]{:S(2)}) collective-permute-start(bf16[368,1152]{1,0:T(8,128)(2,1)S(1)} %fusion.71), channel_id=1, source_target_pairs={{0,1},{1,0},{2,3},{3,2},{4,5},{5,4},{6,7},{7,6},{8,9},{9,8},{10,11... | collective-permute-start | bytes 2543624 | tf_op jit(solution)/shard_map/ppermute | solution.py:67
  441.2 20.1 %collective-permute-start.23 = (bf16[368,1152]{1,0:T(8,128)(2,1)S(1)}, bf16[368,1152]{1,0:T(8,128)(2,1)S(1)}, u32[]{:S(2)}, u32[]{:S(2)}) collective-permute-start(bf16[368,1152]{1,0:T(8,128)(2,1)S(1)} %add_convert_fusion.1), channel_id=1, source_target_pairs={{0,1},{1,0},{2,3},{3,2},{4,5},{5,4},{6,7},{7,6},{8,9},{9,8},{10,11... | collective-permute-start | bytes 2543624 | tf_op jit(solution)/shard_map/ppermute | solution.py:67
  470.3 28.1 %copy-start.7 = (bf16[1,368,1152]{2,1,0:T(8,128)(2,1)S(1)}, bf16[1,368,1152]{2,1,0:T(8,128)(2,1)}, u32[]{:S(2)}) copy-start(bf16[1,368,1152]{2,1,0:T(8,128)(2,1)} %param.19) | copy-start | bytes 2543620
  478.9 19.5 %collective-permute-start.24 = (bf16[368,1152]{1,0:T(8,128)(2,1)}, bf16[368,1152]{1,0:T(8,128)(2,1)}, u32[]{:S(2)}, u32[]{:S(2)}) collective-permute-start(bf16[368,1152]{1,0:T(8,128)(2,1)} %slice.279), channel_id=1, source_target_pairs={{0,1},{1,0},{2,3},{3,2},{4,5},{5,4},{6,7},{7,6},{8,9},{9,8},{10,11... | collective-permute-start | bytes 2543624 | tf_op jit(solution)/shard_map/ppermute | solution.py:67
  498.4 22.4 %slice-start.4 = ((s8[6406144]{0:T(1024)(128)(4,1)}), s8[2211840]{0:T(1024)(128)(4,1)S(1)}, s32[]{:S(2)}) async-start(s8[6406144]{0:T(1024)(128)(4,1)} %bitcast.248), calls=%async_computation.9 | async-start | bytes 4423680
  502.3 18.4 %collective-permute-start.25 = (bf16[368,1152]{1,0:T(8,128)(2,1)S(1)}, bf16[368,1152]{1,0:T(8,128)(2,1)S(1)}, u32[]{:S(2)}, u32[]{:S(2)}) collective-permute-start(bf16[368,1152]{1,0:T(8,128)(2,1)S(1)} %multiply_convert_fusion.3), channel_id=1, source_target_pairs={{0,1},{1,0},{2,3},{3,2},{4,5},{5,4},{6,7},{7,6},{8,9},{9,8},{10,11... | collective-permute-start | bytes 2543624 | tf_op jit(solution)/shard_map/ppermute | solution.py:67
  548.1 17.8 %collective-permute-start.26 = (bf16[368,1152]{1,0:T(8,128)(2,1)}, bf16[368,1152]{1,0:T(8,128)(2,1)}, u32[]{:S(2)}, u32[]{:S(2)}) collective-permute-start(bf16[368,1152]{1,0:T(8,128)(2,1)} %slice.278), channel_id=1, source_target_pairs={{0,1},{1,0},{2,3},{3,2},{4,5},{5,4},{6,7},{7,6},{8,9},{9,8},{10,11... | collective-permute-start | bytes 2543624 | tf_op jit(solution)/shard_map/ppermute | solution.py:67
  572.7 16.7 %collective-permute-start.27 = (bf16[368,1152]{1,0:T(8,128)(2,1)S(1)}, bf16[368,1152]{1,0:T(8,128)(2,1)S(1)}, u32[]{:S(2)}, u32[]{:S(2)}) collective-permute-start(bf16[368,1152]{1,0:T(8,128)(2,1)S(1)} %convert_element_type.165), channel_id=1, source_target_pairs={{0,1},{1,0},{2,3},{3,2},{4,5},{5,4},{6,7},{7,6},{8,9},{9,8},{10,11... | collective-permute-start | bytes 2543624 | tf_op jit(solution)/shard_map/ppermute | solution.py:67
  602.2 47.1 %collective-permute-start.29 = (bf16[2,8,368,72]{2,3,1,0:T(8,128)(2,1)}, bf16[2,8,368,72]{2,3,1,0:T(8,128)(2,1)}, u32[]{:S(2)}, u32[]{:S(2)}) collective-permute-start(bf16[2,8,368,72]{2,3,1,0:T(8,128)(2,1)} %slice.276), channel_id=1, source_target_pairs={{0,2},{2,0},{1,3},{3,1},{4,6},{6,4},{5,7},{7,5},{8,10},{10,8},{9,1... | collective-permute-start | bytes 2543624 | tf_op jit(solution)/shard_map/ppermute | solution.py:67
  640.3 11.3 %collective-permute-start.28 = (bf16[2,8,368,72]{2,3,1,0:T(8,128)(2,1)S(1)}, bf16[2,8,368,72]{2,3,1,0:T(8,128)(2,1)S(1)}, u32[]{:S(2)}, u32[]{:S(2)}) collective-permute-start(bf16[2,8,368,72]{2,3,1,0:T(8,128)(2,1)S(1)} %slice.277), channel_id=1, source_target_pairs={{0,2},{2,0},{1,3},{3,1},{4,6},{6,4},{5,7},{7,5},{8,10},{10,8},{9,1... | collective-permute-start | bytes 2543624 | tf_op jit(solution)/shard_map/ppermute | solution.py:67
  669.0 200.2 %reduce-scatter.5.cloned.1.call-start = ((), (), s32[]{:S(2)}) async-start(), calls=%async_computation.3 | async-start | bytes 10653696 | tf_op jit(solution)/shard_map/reduce_scatter | solution.py:222
  670.4 30.0 %copy-start.2 = (bf16[1,368,1152]{2,1,0:T(8,128)(2,1)S(1)}, bf16[1,368,1152]{2,1,0:T(8,128)(2,1)}, u32[]{:S(2)}) copy-start(bf16[1,368,1152]{2,1,0:T(8,128)(2,1)} %param.18) | copy-start | bytes 2543620
  670.4 30.0 %copy-start.46 = (f32[1152]{0:T(1024)S(1)}, f32[1152]{0:T(1024)}, u32[]{:S(2)}) copy-start(f32[1152]{0:T(1024)} %copy-done.45) | copy-start | bytes 13828
  670.4 30.0 %copy-start.48 = (f32[368]{0:T(512)S(1)}, f32[368]{0:T(512)}, u32[]{:S(2)}) copy-start(f32[368]{0:T(512)} %copy-done.47) | copy-start | bytes 4420
  670.4 30.0 %copy-start.50 = (f32[368]{0:T(512)S(1)}, f32[368]{0:T(512)}, u32[]{:S(2)}) copy-start(f32[368]{0:T(512)} %copy-done.49) | copy-start | bytes 4420
  678.5 24.3 %copy-start.5 = (f32[368,1152]{1,0:T(8,128)S(1)}, f32[368,1152]{1,0:T(8,128)}, u32[]{:S(2)}) copy-start(f32[368,1152]{1,0:T(8,128)} %copy-done.4) | copy-start | bytes 5087236
  679.5 20.9 %collective-permute-start.30 = (bf16[368,1152]{1,0:T(8,128)(2,1)}, bf16[368,1152]{1,0:T(8,128)(2,1)S(1)}, u32[]{:S(2)}, u32[]{:S(2)}) collective-permute-start(bf16[368,1152]{1,0:T(8,128)(2,1)} %fusion.72), channel_id=1, source_target_pairs={{0,1},{1,0},{2,3},{3,2},{4,5},{5,4},{6,7},{7,6},{8,9},{9,8},{10,11... | collective-permute-start | bytes 2543624 | tf_op jit(solution)/shard_map/ppermute | solution.py:67
  704.9 1.3 collective-permute-start.31
  706.2 4.6 collective-permute-start.32
  710.8 5.2 collective-permute-start.33
  713.6 1.2 collective-permute-start.36
  714.8 3.7 collective-permute-start.37
  715.9 13.8 %collective-permute-start.34 = (f32[6913]{0:T(1024)S(1)}, f32[6913]{0:T(1024)S(1)}, u32[]{:S(2)}, u32[]{:S(2)}) collective-permute-start(f32[6913]{0:T(1024)S(1)} %add.445), channel_id=1, source_target_pairs={{0,16},{4,20},{8,24},{12,28},{16,0},{20,4},{24,8},{28,12},{1,17},{... | collective-permute-start | bytes 82964 | tf_op jit(solution)/shard_map/ppermute | solution.py:114
  718.5 5.6 collective-permute-start.38
  724.1 5.6 collective-permute-start.39
  729.8 3.9 collective-permute-start.35
  (48 other events, 363.7 us)
Sparse Core Ops, SparseCore 0:
  10.8 120.2 all-gather.1
  669.1 82.9 reduce-scatter.6
  756.2 112.9 reduce-scatter.4
